TPU v7x, 8 devices: a whole 2x2x1 slice. The times are simulated.
8 devices in a mesh: batch: 1 (over z), y: 2 (over y), x: 4 (over x, core).
Axes of the slice: x: 2, y: 2, z: 1, core: 2. Of those that a mesh axis runs over, the one named last changes fastest.
Arguments:
- field: float32 [512, 512, 64], P(('batch', 'x'), 'y')
- sub_x: float32 [512, 512], P(('batch', 'x'), 'y')
- diag_x: float32 [512, 512], P(('batch', 'x'), 'y')
- sup_x: float32 [512, 512], P(('batch', 'x'), 'y')
- sub_y: float32 [512, 512], P(('batch', 'x'), 'y')
- diag_y: float32 [512, 512], P(('batch', 'x'), 'y')
- sup_y: float32 [512, 512], P(('batch', 'x'), 'y')
Outputs:
- output: float32 [512, 512, 64], P(('batch', 'x'), 'y')
All inputs are finite; a program needn't handle non-finite values.
Results may differ from a plain program's by a relative error of at most 0.001.
Values sent between devices are 32-bit elements.
A program may use at most 1 GiB of HBM per device.

v0:
```python
import jax
import jax.numpy as jnp
from jax import lax
from jax.sharding import PartitionSpec as P


def forward_sweep(sub, diag, sup, rhs, ratio_in, g_in):
    def step(carry, row):
        prev_ratio, prev_g = carry
        sub_row, diag_row, sup_row, rhs_row = row
        pivot = 1.0 + diag_row - sub_row * prev_ratio
        ratio = sup_row / pivot
        g_row = (rhs_row - sub_row[..., None] * prev_g) / pivot[..., None]
        return (ratio, g_row), (ratio, g_row)

    _, (ratios, g_rows) = lax.scan(step, (ratio_in, g_in), (sub, diag, sup, rhs))
    return ratios, g_rows


def backward_sweep(ratios, g_rows, next_in):
    def step(next_val, row):
        ratio, g_row = row
        value = g_row - ratio[..., None] * next_val
        return value, value

    _, solved = lax.scan(step, next_in, (ratios, g_rows), reverse=True)
    return solved


def neighbour_perms(n_dev):
    up_perm = [(i, i + 1) for i in range(n_dev - 1)]
    down_perm = [(i + 1, i) for i in range(n_dev - 1)]
    return up_perm, down_perm


def halo_apply(sub, diag, sup, tile, axis_name, n_dev, along):
    up_perm, down_perm = neighbour_perms(n_dev)
    size = tile.shape[along]
    from_prev = lax.ppermute(lax.slice_in_dim(tile, size - 1, size, axis=along), axis_name, up_perm)
    from_next = lax.ppermute(lax.slice_in_dim(tile, 0, 1, axis=along), axis_name, down_perm)
    minus = jnp.concatenate([from_prev, lax.slice_in_dim(tile, 0, size - 1, axis=along)], axis=along)
    plus = jnp.concatenate([lax.slice_in_dim(tile, 1, size, axis=along), from_next], axis=along)
    return sub[..., None] * minus + diag[..., None] * tile + sup[..., None] * plus


def chain_solve(sub, diag, sup, rhs, axis_name, n_dev):
    my_pos = lax.axis_index(axis_name)
    up_perm, down_perm = neighbour_perms(n_dev)

    def fwd_body(step_pos, state):
        ratio_in, g_in, ratios, g_rows = state
        new_ratios, new_g = lax.cond(my_pos == step_pos, lambda: forward_sweep(sub, diag, sup, rhs, ratio_in, g_in), lambda: (ratios, g_rows))
        sent_ratio = lax.ppermute(new_ratios[-1], axis_name, up_perm)
        sent_g = lax.ppermute(new_g[-1], axis_name, up_perm)
        take = my_pos == step_pos + 1
        ratio_in = jnp.where(take, sent_ratio, ratio_in)
        g_in = jnp.where(take, sent_g, g_in)
        return ratio_in, g_in, new_ratios, new_g

    fwd_start = (jnp.zeros_like(diag[0]), jnp.zeros_like(rhs[0]), jnp.zeros_like(diag), jnp.zeros_like(rhs))
    _, _, ratios, g_rows = lax.fori_loop(0, n_dev, fwd_body, fwd_start)

    def bwd_body(step_pos, state):
        next_in, solved = state
        owner = n_dev - 1 - step_pos
        new_solved = lax.cond(my_pos == owner, lambda: backward_sweep(ratios, g_rows, next_in), lambda: solved)
        sent = lax.ppermute(new_solved[0], axis_name, down_perm)
        next_in = jnp.where(my_pos == owner - 1, sent, next_in)
        return next_in, new_solved

    _, solved = lax.fori_loop(0, n_dev, bwd_body, (jnp.zeros_like(rhs[0]), jnp.zeros_like(rhs)))
    return solved


def solution(mesh):
    n_x = mesh.shape["x"]
    n_y = mesh.shape["y"]
    tile_spec = P(("batch", "x"), "y", None)
    coef_spec = P(("batch", "x"), "y")

    def local_step(field, sub_x, diag_x, sup_x, sub_y, diag_y, sup_y):
        r_one = field - halo_apply(sub_y, diag_y, sup_y, field, "y", n_y, 1)
        half = chain_solve(sub_x, diag_x, sup_x, r_one, "x", n_x)
        r_two = half - halo_apply(sub_x, diag_x, sup_x, half, "x", n_x, 0)
        solved_t = chain_solve(sub_y.T, diag_y.T, sup_y.T, jnp.swapaxes(r_two, 0, 1), "y", n_y)
        return jnp.swapaxes(solved_t, 0, 1)

    return jax.shard_map(local_step, mesh=mesh, in_specs=(tile_spec, coef_spec, coef_spec, coef_spec, coef_spec, coef_spec, coef_spec), out_specs=tile_spec, check_vma=False)
```

profile of v0, /device:TPU:0, one launch (start us, length us, event | category | flops | bytes accessed | tf_op | source)
XLA Modules:
  0.0 5717.7 jit_solution(14709481585852213065)
XLA Ops:
  0.0 12.3 copy.16
  20.3 23.6 fusion.24
  44.6 21.9 fusion.12
  66.6 7.8 broadcast.58.clone
  75.1 1206.9 %while.150 = (s32[]{:T(128)}, f32[256]{0:T(256)S(1)}, f32[256,64]{1,0:T(8,128)S(1)}, f32[128,256]{1,0:T(8,128)}, f32[128,256,64]{2,1,0:T(8,128)}, /*index=5*/s32...) while((s32[]{:T(128)}, f32[256]{0:T(256)S(1)}, ...), condition=%wide.region_5.6_spmd.clone, body=%wide.region_0.5_spmd.clone.sunk | while | flops 100104 | bytes 1142812 | solution.py:61
  75.1 391.6 %conditional.12 = ((f32[128,256]{1,0:T(8,128)}, f32[128,256,64]{2,1,0:T(8,128)})) conditional(s32[]{:T(128)} %convert_element_type.48, (f32[128,256]{1,0:T(8,128)}, f32[128,256,64]{2,1,0:T(8,128)}) %tuple.295, (f32[128,256]{1,0:T(8,128)S(1)}, f32[128,256]{1,0:T(8,128)S(1)}, f32[128,256]{1,0:T(8,128)S(1)}, f32[128,256,64]{2,1,0:T(8,128)}, ...), branch_computations={%region_1.0_spmd, %region_2.4_spmd} | conditional | flops 50178 | bytes 410353 | solution.py:52
  75.2 391.6 %while.146 = (s32[]{:T(128)}, f32[256]{0:T(256)S(1)}, f32[256,64]{1,0:T(8,128)S(1)}, f32[128,256]{1,0:T(8,128)}, f32[128,256,64]{2,1,0:T(8,128)}, /*index=5*/f32...) while((s32[]{:T(128)}, f32[256]{0:T(256)S(1)}, ...), condition=%wide.region_4.3_spmd, body=%wide.region_3.2_spmd.sunk | while | flops 50178 | bytes 410233 | solution.py:16
  472.8 393.9 %collective-permute-start.4 = (f32[256]{0:T(256)S(1)}, f32[256]{0:T(256)S(1)}, u32[]{:S(2)}, u32[]{:S(2)}) collective-permute-start(f32[256]{0:T(256)S(1)} %bitcast.111), channel_id=1, source_target_pairs={{0,1},{1,2},{2,3},{4,5},{5,6},{6,7}} | collective-permute-start | bytes 3080 | tf_op jit(solution)/shard_map/while/body/eval_jaxpr/ppermute | solution.py:53
  875.1 396.0 %collective-permute-start.5 = (f32[256,64]{1,0:T(8,128)S(1)}, f32[256,64]{1,0:T(8,128)S(1)}, u32[]{:S(2)}, u32[]{:S(2)}) collective-permute-start(f32[256,64]{1,0:T(8,128)S(1)} %slice_bitcast_fusion.10), channel_id=1, source_target_pairs={{0,1},{1,2},{2,3},{4,5},{5,6},{6,7}} | collective-permute-start | bytes 196616 | tf_op jit(solution)/shard_map/while/body/eval_jaxpr/ppermute | solution.py:54
  1282.0 7.9 broadcast.58
  1289.9 1654.0 %while.151 = (s32[]{:T(128)}, f32[256,64]{1,0:T(8,128)S(1)}, f32[128,256,64]{2,1,0:T(8,128)}, s32[]{:T(128)}, f32[128,256,64]{2,1,0:T(8,128)}, /*index=5*/f32[12...) while((s32[]{:T(128)}, f32[256,64]{1,0:T(8,128)S(1)}, f32[128,256,64]{2,1,0:T(8,128)}, ...), condition=%wide.region_11.12_spmd.clone, body=%wide.region_6.11_spmd.clone.sunk | while | flops 81931 | bytes 9506189 | solution.py:71
  1292.1 391.0 %collective-permute-done.3 = f32[256,64]{1,0:T(8,128)S(1)} collective-permute-done((f32[256,64]{1,0:T(8,128)S(1)}, f32[256,64]{1,0:T(8,128)S(1)}, u32[]{:S(2)}, u32[]{:S(2)}) %collective-permute-start.3) | collective-permute-done | bytes 65568 | tf_op jit(solution)/shard_map/while/body/eval_jaxpr/ppermute | solution.py:67
  1685.5 5.7 collective-permute-done.3
  1693.5 934.0 %collective-permute-done.3 = f32[256,64]{1,0:T(8,128)S(1)} collective-permute-done((f32[256,64]{1,0:T(8,128)S(1)}, f32[256,64]{1,0:T(8,128)S(1)}, u32[]{:S(2)}, u32[]{:S(2)}) %collective-permute-start.3) | collective-permute-done | bytes 65568 | tf_op jit(solution)/shard_map/while/body/eval_jaxpr/ppermute | solution.py:67
  2627.5 312.1 %conditional.13 = (f32[128,256,64]{2,1,0:T(8,128)}) conditional(s32[]{:T(128)} %convert_element_type.49, f32[128,256,64]{2,1,0:T(8,128)} %get-tuple-element.1978, (f32[128,256,64]{2,1,0:T(8,128)}, f32[128,256]{1,0:T(8,128)}, f32[256,64]{1,0:T(8,128)S(1)}) %tuple.298), branch_computations={%region_7.7_spmd, %region_8.10_spmd} | conditional | flops 32771 | bytes 8785069 | solution.py:66
  2627.6 7.9 broadcast.43
  2635.4 304.2 %while.147 = (s32[]{:T(128)}, f32[256,64]{1,0:T(8,128)S(1)}, f32[128,256,64]{2,1,0:T(8,128)}, f32[128,256,64]{2,1,0:T(8,128)}, f32[128,256]{1,0:T(8,128)}, /*index=5*/s32[]{:T(128)}, s32[]{:T(128)}) while((s32[]{:T(128)}, f32[256,64]{1,0:T(8,128)S(1)}, f32[128,256,64]{2,1,0:T(8,128)}, f32[128,256,64]{2,1,0:T(8,128)}, f32[128,256]{1,0:T(8,128)}, ...), condition=%wide.region_10.9_spmd, body=%wide.region_9.8_spmd.sunk | while | flops 32771 | bytes 396385 | solution.py:26
  2943.8 19.2 copy.25
  2966.6 23.9 fusion.22
  2990.5 25.4 fusion.16
  3016.0 7.9 broadcast.55.clone
  3024.5 1491.8 %while.152 = (s32[]{:T(128)}, f32[128]{0:T(128)S(1)}, f32[128,64]{1,0:T(8,128)S(1)}, f32[256,128]{1,0:T(8,128)}, f32[256,128,64]{2,1,0:T(8,128)}, /*index=5*/s32...) while((s32[]{:T(128)}, f32[128]{0:T(128)S(1)}, ...), condition=%wide.region_17.18_spmd.clone, body=%wide.region_12.17_spmd.clone.sunk | while | flops 50056 | bytes 569368 | solution.py:61
  3024.6 738.2 %conditional.14 = ((f32[256,128]{1,0:T(8,128)}, f32[256,128,64]{2,1,0:T(8,128)})) conditional(s32[]{:T(128)} %convert_element_type.50, (f32[256,128]{1,0:T(8,128)}, f32[256,128,64]{2,1,0:T(8,128)}) %tuple.300, (f32[256,128]{1,0:T(8,128)S(1)}, f32[256,128]{1,0:T(8,128)S(1)}, f32[256,128]{1,0:T(8,128)S(1)}, f32[256,128,64]{2,1,0:T(8,128)}, ...), branch_computations={%region_13.13_spmd, %region_14.16_spmd} | conditional | flops 25090 | bytes 202989 | solution.py:52
  3024.6 738.2 %while.148 = (s32[]{:T(128)}, f32[128]{0:T(128)S(1)}, f32[128,64]{1,0:T(8,128)S(1)}, f32[256,128]{1,0:T(8,128)}, f32[256,128,64]{2,1,0:T(8,128)}, /*index=5*/f32...) while((s32[]{:T(128)}, f32[128]{0:T(128)S(1)}, ...), condition=%wide.region_16.15_spmd, body=%wide.region_15.14_spmd.sunk | while | flops 25090 | bytes 202869 | solution.py:16
  3769.7 742.6 %collective-permute-start.1 = (f32[128]{0:T(128)S(1)}, f32[128]{0:T(128)S(1)}, u32[]{:S(2)}, u32[]{:S(2)}) collective-permute-start(f32[128]{0:T(128)S(1)} %slice_bitcast_fusion.12), channel_id=1, source_target_pairs={{0,4},{1,5},{2,6},{3,7}} | collective-permute-start | bytes 1544 | tf_op jit(solution)/shard_map/while/body/eval_jaxpr/ppermute | solution.py:53
  4516.3 7.9 broadcast.55
  4524.2 1179.4 %while.153 = (s32[]{:T(128)}, f32[128,64]{1,0:T(8,128)S(1)}, f32[256,128,64]{2,1,0:T(8,128)}, s32[]{:T(128)}, f32[256,128,64]{2,1,0:T(8,128)}, /*index=5*/f32[256,128]{1,0:T(8,128)}, s32[]{:T(128)}, s32[]{:T(128)}) while((s32[]{:T(128)}, f32[128,64]{1,0:T(8,128)S(1)}, f32[256,128,64]{2,1,0:T(8,128)}, s32[]{:T(128)}, ...), condition=%wide.region_23.24_spmd.clone, body=%wide.region_18.23_spmd.clone.sunk | while | flops 40971 | bytes 8947581 | solution.py:71
  4526.4 587.3 %collective-permute-done = f32[128,64]{1,0:T(8,128)S(1)} collective-permute-done((f32[128,64]{1,0:T(8,128)S(1)}, f32[128,64]{1,0:T(8,128)S(1)}, u32[]{:S(2)}, u32[]{:S(2)}) %collective-permute-start) | collective-permute-done | bytes 32800 | tf_op jit(solution)/shard_map/while/body/eval_jaxpr/ppermute | solution.py:67
  5113.8 582.8 %conditional.15 = (f32[256,128,64]{2,1,0:T(8,128)}) conditional(s32[]{:T(128)} %convert_element_type.51, f32[256,128,64]{2,1,0:T(8,128)} %get-tuple-element.2042, (f32[256,128,64]{2,1,0:T(8,128)}, f32[256,128]{1,0:T(8,128)}, f32[128,64]{1,0:T(8,128)S(1)}) %tuple.303), branch_computations={%region_19.19_spmd, %region_20.22_spmd} | conditional | flops 16387 | bytes 8586925 | solution.py:66
  5113.8 7.9 broadcast.47
  5121.7 574.9 %while.149 = (s32[]{:T(128)}, f32[128,64]{1,0:T(8,128)S(1)}, f32[256,128,64]{2,1,0:T(8,128)}, f32[256,128,64]{2,1,0:T(8,128)}, f32[256,128]{1,0:T(8,128)}, /*index=5*/s32[]{:T(128)}, s32[]{:T(128)}) while((s32[]{:T(128)}, f32[128,64]{1,0:T(8,128)S(1)}, f32[256,128,64]{2,1,0:T(8,128)}, f32[256,128,64]{2,1,0:T(8,128)}, ...), condition=%wide.region_22.21_spmd, body=%wide.region_21.20_spmd.sunk | while | flops 16387 | bytes 198241 | solution.py:26
  5703.6 14.1 copy.26
  (2309 shorter events, 2076.6 us)
Async XLA Ops:
  13.6 31.1 collective-permute-start.6
  18.8 25.1 copy-start.6
  18.9 25.2 copy-start.5
  18.9 25.3 copy-start.4
  18.9 25.4 copy-start.1
  18.9 25.5 copy-start.2
  18.9 25.6 copy-start.3
  18.9 25.7 collective-permute-start.7
  467.5 3.5 collective-permute-start.4
  469.7 2.3 collective-permute-start.5
  472.8 396.8 %collective-permute-start.4 = (f32[256]{0:T(256)S(1)}, f32[256]{0:T(256)S(1)}, u32[]{:S(2)}, u32[]{:S(2)}) collective-permute-start(f32[256]{0:T(256)S(1)} %bitcast.111), channel_id=1, source_target_pairs={{0,1},{1,2},{2,3},{4,5},{5,6},{6,7}} | collective-permute-start | bytes 3080 | tf_op jit(solution)/shard_map/while/body/eval_jaxpr/ppermute | solution.py:53
  867.6 2.9 collective-permute-start.5
  871.3 399.8 %collective-permute-start.4 = (f32[256]{0:T(256)S(1)}, f32[256]{0:T(256)S(1)}, u32[]{:S(2)}, u32[]{:S(2)}) collective-permute-start(f32[256]{0:T(256)S(1)} %bitcast.111), channel_id=1, source_target_pairs={{0,1},{1,2},{2,3},{4,5},{5,6},{6,7}} | collective-permute-start | bytes 3080 | tf_op jit(solution)/shard_map/while/body/eval_jaxpr/ppermute | solution.py:53
  875.1 397.0 %collective-permute-start.5 = (f32[256,64]{1,0:T(8,128)S(1)}, f32[256,64]{1,0:T(8,128)S(1)}, u32[]{:S(2)}, u32[]{:S(2)}) collective-permute-start(f32[256,64]{1,0:T(8,128)S(1)} %slice_bitcast_fusion.10), channel_id=1, source_target_pairs={{0,1},{1,2},{2,3},{4,5},{5,6},{6,7}} | collective-permute-start | bytes 196616 | tf_op jit(solution)/shard_map/while/body/eval_jaxpr/ppermute | solution.py:54
  1272.8 8.2 collective-permute-start.4
  1276.6 5.3 collective-permute-start.5
  1290.8 392.3 %collective-permute-start.3 = (f32[256,64]{1,0:T(8,128)S(1)}, f32[256,64]{1,0:T(8,128)S(1)}, u32[]{:S(2)}, u32[]{:S(2)}) collective-permute-start(f32[256,64]{1,0:T(8,128)S(1)} %slice_bitcast_fusion.11), channel_id=1, source_target_pairs={{1,0},{2,1},{3,2},{5,4},{6,5},{7,6}} | collective-permute-start | bytes 196616 | tf_op jit(solution)/shard_map/while/body/eval_jaxpr/ppermute | solution.py:67
  1684.1 7.0 collective-permute-start.3
  1692.2 935.3 %collective-permute-start.3 = (f32[256,64]{1,0:T(8,128)S(1)}, f32[256,64]{1,0:T(8,128)S(1)}, u32[]{:S(2)}, u32[]{:S(2)}) collective-permute-start(f32[256,64]{1,0:T(8,128)S(1)} %slice_bitcast_fusion.11), channel_id=1, source_target_pairs={{1,0},{2,1},{3,2},{5,4},{6,5},{7,6}} | collective-permute-start | bytes 196616 | tf_op jit(solution)/shard_map/while/body/eval_jaxpr/ppermute | solution.py:67
  2940.5 3.2 collective-permute-start.3
  2943.8 19.2 copy-start
  2963.1 27.5 collective-permute-start.8
  2965.1 25.4 collective-permute-start.9
  3763.5 3.4 collective-permute-start.1
  3765.6 3.3 collective-permute-start.2
  3769.7 744.7 %collective-permute-start.1 = (f32[128]{0:T(128)S(1)}, f32[128]{0:T(128)S(1)}, u32[]{:S(2)}, u32[]{:S(2)}) collective-permute-start(f32[128]{0:T(128)S(1)} %slice_bitcast_fusion.12), channel_id=1, source_target_pairs={{0,4},{1,5},{2,6},{3,7}} | collective-permute-start | bytes 1544 | tf_op jit(solution)/shard_map/while/body/eval_jaxpr/ppermute | solution.py:53
  4513.1 3.2 collective-permute-start.2
  4525.1 588.6 %collective-permute-start = (f32[128,64]{1,0:T(8,128)S(1)}, f32[128,64]{1,0:T(8,128)S(1)}, u32[]{:S(2)}, u32[]{:S(2)}) collective-permute-start(f32[128,64]{1,0:T(8,128)S(1)} %slice_bitcast_fusion.14), channel_id=1, source_target_pairs={{4,0},{5,1},{6,2},{7,3}} | collective-permute-start | bytes 98312 | tf_op jit(solution)/shard_map/while/body/eval_jaxpr/ppermute | solution.py:67
  5697.5 6.1 collective-permute-start
where the time goes:
time: 5770 us; the launch traced here: 5720 us
  waiting for transfers between devices  1930 us (33%)
  starting transfers between devices  1570 us (27%)
  other arithmetic  1290 us (22%)
  local copies, waits for them, and re-layouts  923 us (16%)
    ppermute x6, waiting for transfers between devices, bwd_body(): sent = lax.ppermute(new_solved[0], axis_name, down_perm)  1920 us
    dynamic_update_slice x768, other arithmetic, forward_sweep(): lax.scan(step, (ratio_in, g_in), (sub, diag, sup, rhs))  1240 us
    ppermute x6, starting transfers between devices, fwd_body(): sent_ratio = lax.ppermute(new_ratios[-1], axis_name, up_perm)  1140 us
    dynamic_update_slice x384, local copies, waits for them, and re-layouts, forward_sweep(): lax.scan(step, (ratio_in, g_in), (sub, diag, sup, rhs))  497 us
    ppermute x6, starting transfers between devices, fwd_body(): sent_g = lax.ppermute(new_g[-1], axis_name, up_perm)  406 us
    mul x256, local copies, waits for them, and re-layouts, step(): value = g_row - ratio[..., None] * next_val  177 us
  transfers between devices with their start and end apart: 22, of which 12 were waited for; matrix products, arithmetic and copies ran while one was open for 1% of the time, Pallas kernels for 0%

commit v1 on v0

v1 whole, which is shorter than its diff:
```python
import functools

import jax
import jax.numpy as jnp
from jax import lax
from jax.experimental import pallas as pl
from jax.experimental.pallas import tpu as pltpu
from jax.sharding import PartitionSpec as P

MESH = pl.DeviceIdType.MESH
NI, NF, NJ = 128, 64, 256
L, S = 128, 8
FB = NF // S
JB = NJ // L
CH = 4
CB = FB // CH
CV = CB * JB
HR = 8
f32 = jnp.float32


def bcast(ref, row):
    return jnp.broadcast_to(ref[pl.ds(row, 1), :], (S, L))


def bcast_x(ref, row, jb):
    return jnp.broadcast_to(ref[jb, pl.ds(row, 1), :], (S, L))


def reduce_kernel(u_hbm, sub_x, diag_x, sup_x, sub_y, diag_y, sup_y,
                  g_out, edge_out, ratio_out,
                  b1, b2, b3, halo_send, halo_recv,
                  low_x, cen_x, high_x, inv_x, s_x, p_x, f_x, q_x,
                  cen_t, lo_t, hi_t, b_t, a_t, c_t, inv_t, s_t,
                  coef_send, coef_recv, mu_send, mu_recv,
                  fl_send, fl_recv, lam_send, lam_recv, wprev, wnext,
                  yl_send, yl_recv,
                  in_sem, halo_ss, halo_rs, coef_ss, coef_rs, mu_ss, mu_rs,
                  fl_ss, fl_rs, lam_ss, lam_rs, y_ss, y_rs):
    my_x = lax.axis_index("x")
    my_y = lax.axis_index("y")
    core = lax.rem(my_x, 2)
    chip = my_x // 2
    mate = {"x": my_x + 1 - 2 * core}
    across = {"x": lax.rem(my_x + 2, 4)}
    beside = {"y": 1 - my_y}
    first_core = core == 0
    first_chip = chip == 0
    first_y = my_y == 0

    barrier = pltpu.get_barrier_semaphore()
    for peer in (mate, across, beside):
        pl.semaphore_signal(barrier, inc=1, device_id=peer, device_id_type=MESH)

    def in_copy(fb, jb):
        k = fb * JB + jb
        return pltpu.make_async_copy(
            u_hbm.at[:, pl.ds(fb * S, S), pl.ds(jb * L, L)], b1.at[k], in_sem.at[k])

    for fb in range(FB):
        for jb in range(JB):
            in_copy(fb, jb).start()

    for jb in range(JB):
        cols = slice(jb * L, (jb + 1) * L)
        d = diag_y[:, cols].T
        lo = sub_y[:, cols].T
        hi = sup_y[:, cols].T
        cen_t[cols, :] = 1.0 - d
        b_t[cols, :] = 1.0 + d
        lo_t[cols, :] = lo
        hi_t[cols, :] = hi
        a_t[cols, :] = jnp.where(first_y, lo, hi)
        c_t[cols, :] = jnp.where(first_y, hi, lo)

    for jb in range(JB):
        cols = slice(jb * L, (jb + 1) * L)
        low_x[jb] = sub_x[:, cols]
        cen_x[jb] = 1.0 + diag_x[:, cols]
        high_x[jb] = sup_x[:, cols]

    def x_factor(i, state):
        row = pl.ds(i, 1)
        out = []
        for jb in range(JB):
            p_prev, f_prev, q, e_sum = state[jb]
            sub, sup = low_x[jb, row, :], high_x[jb, row, :]
            inv = 1.0 / (cen_x[jb, row, :] - sub * p_prev)
            p, s = sup * inv, sub * inv
            fill = -s * f_prev
            inv_x[jb, row, :] = inv
            s_x[jb, row, :] = s
            p_x[jb, row, :] = p
            f_x[jb, row, :] = fill
            q_x[jb, row, :] = q
            out.append((p, fill, -q * p, e_sum + q * fill))
        return tuple(out)

    none = jnp.zeros((1, L), f32)
    ends = lax.fori_loop(0, NI, x_factor, ((none, none + 1.0, none + 1.0, none),) * JB)
    for jb in range(JB):
        p_last, f_last, q_all, e_sum = ends[jb]
        for r, value in enumerate((e_sum, f_last, q_all, -p_last)):
            coef_send[jb, r:r + 1, :] = value
        coef_send[jb, 4:8, :] = jnp.zeros((4, L), f32)

    def y_factor(t, p_prev):
        j = jnp.where(first_y, t, NJ - 1 - t)
        row = pl.ds(j, 1)
        low = a_t[row, :]
        inv = 1.0 / (b_t[row, :] - low * p_prev)
        p = c_t[row, :] * inv
        inv_t[row, :] = inv
        s_t[row, :] = low * inv
        ratio_out[row, :] = p
        return p

    p_end = lax.fori_loop(0, NJ, y_factor, jnp.zeros((1, L), f32))

    pl.semaphore_wait(barrier, 3)

    coef_copy = pltpu.make_async_remote_copy(
        coef_send, coef_recv, coef_ss, coef_rs, device_id=mate, device_id_type=MESH)
    coef_copy.start()

    def halo_copy(fb):
        rows = pl.ds(pl.multiple_of(fb * S, S), S)
        return pltpu.make_async_remote_copy(
            halo_send.at[rows, :], halo_recv.at[rows, :], halo_ss.at[fb], halo_rs.at[fb],
            device_id=beside, device_id_type=MESH)

    def to_columns(fb, _):
        for jb in range(JB):
            in_copy(fb, jb).wait()
        views = [b1.at[fb * JB + jb].reshape(NI * S, L) for jb in range(JB)]
        for f in range(S):
            parts = [views[jb][pl.ds(f, NI, stride=S), :].T for jb in range(JB)]
            for jb in range(JB):
                b2[fb * S + f, HR + jb * L:HR + (jb + 1) * L, :] = parts[jb]
            halo_send[pl.ds(fb * S + f, 1), :] = jnp.where(
                first_y, parts[JB - 1][L - 1:L, :], parts[0][0:1, :])
        halo_copy(fb).start()
        return 0

    lax.fori_loop(0, FB, to_columns, 0)

    def stencil(fi, fb):
        f_all = fb * S + fi
        halo = halo_recv[pl.ds(f_all, 1), :]
        none = jnp.zeros_like(halo)
        b2[f_all, HR - 1:HR, :] = jnp.where(first_y, none, halo)
        b2[f_all, HR + NJ:HR + NJ + 1, :] = jnp.where(first_y, halo, none)
        for jb in range(JB):
            base = HR + jb * L
            cols = slice(jb * L, (jb + 1) * L)
            before = b2[f_all, base - 1:base - 1 + L, :]
            here = b2[f_all, base:base + L, :]
            after = b2[f_all, base + 1:base + 1 + L, :]
            r = cen_t[cols, :] * here - lo_t[cols, :] * before - hi_t[cols, :] * after
            b1.at[fb * JB + jb].reshape(NI * S, L)[pl.ds(fi, NI, stride=S), :] = r.T
        return fb

    def fl_copy(c):
        return pltpu.make_async_remote_copy(
            fl_send.at[c], fl_recv.at[c], fl_ss.at[c], fl_rs.at[c], device_id=mate, device_id_type=MESH)

    def lam_copy(c):
        return pltpu.make_async_remote_copy(
            lam_send.at[c], lam_recv.at[c], lam_ss.at[c], lam_rs.at[c], device_id=across, device_id_type=MESH)

    mu_copy = pltpu.make_async_remote_copy(
        mu_send, mu_recv, mu_ss, mu_rs, device_id=across, device_id_type=MESH)

    def x_forward(c):
        def step(i, state):
            gs, accs = state
            inv = [bcast_x(inv_x, i, jb) for jb in range(JB)]
            s = [bcast_x(s_x, i, jb) for jb in range(JB)]
            q = [bcast_x(q_x, i, jb) for jb in range(JB)]
            new_g, new_acc = [], []
            for v in range(CV):
                jb = v % JB
                g = b1[c * CV + v, i] * inv[jb] - s[jb] * gs[v]
                b3[c * CV + v, i] = g
                new_g.append(g)
                new_acc.append(accs[v] + q[jb] * g)
            return tuple(new_g), tuple(new_acc)

        zeros = tuple(jnp.zeros((S, L), f32) for _ in range(CV))
        gs, accs = lax.fori_loop(0, NI, step, (zeros, zeros), unroll=4)
        for v in range(CV):
            fl_send[c, 0, v] = accs[v]
            fl_send[c, 1, v] = gs[v]
        fl_copy(c).start()

    def pair_coefs(jb):
        def both(row):
            mine, other = coef_send[jb, row:row + 1, :], coef_recv[jb, row:row + 1, :]
            return jnp.where(first_core, mine, other), jnp.where(first_core, other, mine)

        ef, el, qf, ql = both(0), both(1), both(2), both(3)
        return ef, el, qf, ql, 1.0 / (1.0 - ql[0] * ef[1])

    def own_mu(jb):
        ef, el, qf, ql, det = pair_coefs(jb)
        return jnp.where(first_chip, el[1] * det * ql[0] * qf[1] + ql[1], ef[0] + qf[0] * ef[1] * det * el[0])

    def up(row):
        return jnp.broadcast_to(row, (S, L))

    def pair_data(c, v):
        f_mine, f_other = fl_send[c, 0, v], fl_recv[c, 0, v]
        l_mine, l_other = fl_send[c, 1, v], fl_recv[c, 1, v]
        f0, f1 = jnp.where(first_core, f_mine, f_other), jnp.where(first_core, f_other, f_mine)
        l0, l1 = jnp.where(first_core, l_mine, l_other), jnp.where(first_core, l_other, l_mine)
        return f0, f1, l0, l1

    def merge(c):
        fl_copy(c).wait_recv()
        for v in range(CV):
            ef, el, qf, ql, det = pair_coefs(v % JB)
            f0, f1, l0, l1 = pair_data(c, v)
            last0 = up(det) * (l0 + up(ql[0]) * f1)
            first1 = f1 + up(ef[1]) * last0
            lam_send[c, v] = jnp.where(first_chip, l1 + up(el[1]) * last0, f0 + up(qf[0]) * first1)
        lam_copy(c).start()

    def settle(c):
        lam_copy(c).wait_recv()
        for v in range(CV):
            jb = v % JB
            ef, el, qf, ql, det = pair_coefs(jb)
            f0, f1, l0, l1 = pair_data(c, v)
            mu_mine, mu_other = mu_send[jb], mu_recv[jb]
            mid = (lam_recv[c, v] + mu_other * lam_send[c, v]) / (1.0 - mu_mine * mu_other)
            zero = jnp.zeros_like(mid)
            prev, nxt = jnp.where(first_chip, zero, mid), jnp.where(first_chip, mid, zero)
            rest = f1 + up(qf[1]) * nxt
            last0 = up(det) * (l0 + up(el[0]) * prev + up(ql[0]) * rest)
            first1 = rest + up(ef[1]) * last0
            wprev[c, v] = jnp.where(first_core, prev, last0)
            wnext[c, v] = jnp.where(first_core, first1, nxt)

    def x_backward(c):
        prevs = [wprev[c, v] for v in range(CV)]

        def step(t, ws):
            i = NI - 1 - t
            fill = [bcast_x(f_x, i, jb) for jb in range(JB)]
            p = [bcast_x(p_x, i, jb) for jb in range(JB)]
            out = []
            for v in range(CV):
                jb = v % JB
                w = b3[c * CV + v, i] + fill[jb] * prevs[v] - p[jb] * ws[v]
                b1[c * CV + v, i] = w + (w - b1[c * CV + v, i])
                out.append(w)
            return tuple(out)

        lax.fori_loop(0, NI, step, tuple(wnext[c, v] for v in range(CV)), unroll=4)

    def turn(fb):
        for jb in range(JB):
            view = b1.at[fb * JB + jb].reshape(NI * S, L)
            for f in range(S):
                g_out[fb, pl.ds(jb * L * S + f, L, stride=S), :] = view[pl.ds(f, NI, stride=S), :].T

    for c in range(CH):
        for fb in range(c * CB, (c + 1) * CB):
            halo_copy(fb).wait_recv()
            lax.fori_loop(0, S, stencil, fb, unroll=4)
        x_forward(c)
        if c == 0:
            coef_copy.wait_recv()
            for jb in range(JB):
                mu_send[jb] = up(own_mu(jb))
            mu_copy.start()
        else:
            merge(c - 1)
    merge(CH - 1)
    mu_copy.wait_recv()
    for c in range(CH):
        settle(c)
        x_backward(c)
        for fb in range(c * CB, (c + 1) * CB):
            turn(fb)

    def y_forward(t, gs):
        j = jnp.where(first_y, t, NJ - 1 - t)
        inv, s = bcast(inv_t, j), bcast(s_t, j)
        rows = pl.ds(pl.multiple_of(j * S, S), S)
        out = []
        for fb in range(FB):
            g = g_out[fb, rows, :] * inv - s * gs[fb]
            g_out[fb, rows, :] = g
            out.append(g)
        return tuple(out)

    gs = lax.fori_loop(0, NJ, y_forward, tuple(jnp.zeros((S, L), f32) for _ in range(FB)), unroll=4)
    for fb in range(FB):
        yl_send[fb] = gs[fb]
    yl_send[FB] = up(-p_end)
    y_copy = pltpu.make_async_remote_copy(
        yl_send, yl_recv, y_ss, y_rs, device_id=beside, device_id_type=MESH)
    y_copy.start()
    y_copy.wait_recv()
    mu_mine, mu_other = yl_send[FB], yl_recv[FB]
    scale = 1.0 / (1.0 - mu_mine * mu_other)
    for fb in range(FB):
        edge_out[fb] = (yl_recv[fb] + mu_other * yl_send[fb]) * scale

    y_copy.wait_send()
    coef_copy.wait_send()
    mu_copy.wait_send()
    for fb in range(FB):
        halo_copy(fb).wait_send()
    for c in range(CH):
        fl_copy(c).wait_send()
        lam_copy(c).wait_send()


OB = 4


def finish_kernel(g_ref, edge_ref, ratio_ref, out_hbm, buf, out_sem):
    first_y = lax.axis_index("y") == 0

    def out_copy(fb, jb):
        k = fb * JB + jb
        return pltpu.make_async_copy(
            buf.at[k], out_hbm.at[:, pl.ds(fb * S, S), pl.ds(jb * L, L)], out_sem.at[k])

    for start in range(0, FB, OB):
        fbs = range(start, start + OB)

        def y_backward(t, ws):
            j = jnp.where(first_y, NJ - 1 - t, t)
            p = bcast(ratio_ref, j)
            rows = pl.ds(pl.multiple_of(j * S, S), S)
            out = []
            for fb, w in zip(fbs, ws):
                w = g_ref[fb, rows, :] - p * w
                g_ref[fb, rows, :] = w
                out.append(w)
            return tuple(out)

        lax.fori_loop(0, NJ, y_backward, tuple(edge_ref[fb] for fb in fbs), unroll=4)
        for fb in fbs:
            for jb in range(JB):
                view = buf.at[fb * JB + jb].reshape(NI * S, L)
                for f in range(S):
                    view[pl.ds(f, NI, stride=S), :] = g_ref[fb, pl.ds(jb * L * S + f, L, stride=S), :].T
                out_copy(fb, jb).start()
    for fb in range(FB):
        for jb in range(JB):
            out_copy(fb, jb).wait()


def solution(mesh):
    tile_spec = P(("batch", "x"), "y", None)
    coef_spec = P(("batch", "x"), "y")
    vmem = pl.BlockSpec(memory_space=pltpu.VMEM)
    hbm = pl.BlockSpec(memory_space=pl.ANY)
    V, DMA = pltpu.VMEM, pltpu.SemaphoreType.DMA
    row_x, col_t = V((JB, NI, L), f32), V((NJ, NI), f32)

    def local_step(field, *coefs):
        g, edge, ratio = pl.pallas_call(
            reduce_kernel,
            out_shape=(jax.ShapeDtypeStruct((FB, NJ * S, L), f32),
                       jax.ShapeDtypeStruct((FB, S, L), f32),
                       jax.ShapeDtypeStruct((NJ, L), f32)),
            in_specs=[hbm] + [vmem] * 6,
            out_specs=(vmem, vmem, vmem),
            scratch_shapes=[
                V((FB * JB, NI, S, L), f32), V((NF, NJ + 2 * HR, L), f32), V((FB * JB, NI, S, L), f32),
                V((NF, L), f32), V((NF, L), f32),
                row_x, row_x, row_x, row_x, row_x, row_x, row_x, row_x,
                col_t, col_t, col_t, col_t, col_t, col_t, col_t, col_t,
                V((JB, S, L), f32), V((JB, S, L), f32), V((JB, S, L), f32), V((JB, S, L), f32),
                V((CH, 2, CV, S, L), f32), V((CH, 2, CV, S, L), f32),
                V((CH, CV, S, L), f32), V((CH, CV, S, L), f32),
                V((CH, CV, S, L), f32), V((CH, CV, S, L), f32),
                V((FB + 1, S, L), f32), V((FB + 1, S, L), f32),
                DMA((FB * JB,)), DMA((FB,)), DMA((FB,)), DMA, DMA, DMA, DMA,
                DMA((CH,)), DMA((CH,)), DMA((CH,)), DMA((CH,)), DMA, DMA,
            ],
            compiler_params=pltpu.CompilerParams(
                collective_id=0, has_side_effects=True, vmem_limit_bytes=50 << 20),
            name="reduce",
        )(jnp.swapaxes(field, 1, 2), *coefs)
        out = pl.pallas_call(
            finish_kernel,
            out_shape=jax.ShapeDtypeStruct((NI, NF, NJ), f32),
            in_specs=[vmem, vmem, vmem],
            out_specs=hbm,
            scratch_shapes=[V((FB * JB, NI, S, L), f32), DMA((FB * JB,))],
            compiler_params=pltpu.CompilerParams(vmem_limit_bytes=30 << 20),
            name="finish",
        )(g, edge, ratio)
        return jnp.swapaxes(out, 1, 2)

    return jax.shard_map(local_step, mesh=mesh, in_specs=(tile_spec,) + (coef_spec,) * 6,
                         out_specs=tile_spec, check_vma=False)
```

time: 5770 us -> 48 us (0.01)
  waiting for transfers between devices: 1930 us -> 0 us
  starting transfers between devices: 1570 us -> 0 us
  other arithmetic: 1290 us -> 0 us
  local copies, waits for them, and re-layouts: 923 us -> 8.8 us
    ppermute x22 -> x0, waiting for transfers between devices: 1930 us -> none  [the longest x6 1920 us: bwd_body(): sent = lax.ppermute(new_solved[0], axis_name, down_perm)]
    ppermute x22 -> x0, starting transfers between devices: 1570 us -> none  [the longest x6 1140 us: fwd_body(): sent_ratio = lax.ppermute(new_ratios[-1], axis_name, up_perm)]
    dynamic_update_slice x768 -> x0, other arithmetic: 1240 us -> none  [forward_sweep(): lax.scan(step, (ratio_in, g_in), (sub, diag, sup, rhs))]
    dynamic_update_slice x384 -> x0, local copies, waits for them, and re-layouts: 497 us -> none  [forward_sweep(): lax.scan(step, (ratio_in, g_in), (sub, diag, sup, rhs))]
    mul x256 -> x0, local copies, waits for them, and re-layouts: 177 us -> none  [step(): value = g_row - ratio[..., None] * next_val]
    dynamic_slice x256 -> x0, local copies, waits for them, and re-layouts: 90.5 us -> none  [forward_sweep(): lax.scan(step, (ratio_in, g_in), (sub, diag, sup, rhs))]
  transfers between devices with their start and end apart: 22 -> 0, of which waited for: 12 -> 0; matrix products, arithmetic and copies ran while one was open for 1% -> 0% of each run, Pallas kernels for 0% -> 0%
where the time goes in v1:
time: 48 us; the launch traced here: 47.8 us
  Pallas kernels  39 us (81%)
  local copies, waits for them, and re-layouts  8.8 us (18%)
    pallas_call x1, Pallas kernels, local_step(): pl.pallas_call(reduce_kernel, out_shape=(jax.ShapeDtypeStruct((FB, NJ * S...  32.8 us
    unnamed x14, local copies, waits for them, and re-layouts  8.8 us
    pallas_call x1, Pallas kernels, local_step(): pl.pallas_call(finish_kernel, out_shape=jax.ShapeDtypeStruct((NI, NF, NJ)...  6.21 us

profile of v1, /device:TPU:0, one launch (start us, length us, event | category | flops | bytes accessed | tf_op | source)
XLA Modules:
  0.0 47.8 jit_solution(1048588697185831197)
XLA Ops:
  0.0 0.0 copy-start.1
  0.0 0.9 %copy-done.1 = f32[128,256]{1,0:T(8,128)S(1)} copy-done((f32[128,256]{1,0:T(8,128)S(1)}, f32[128,256]{1,0:T(8,128)}, u32[]{:S(2)}) %copy-start.1) | copy-done | bytes 131096
  0.9 0.0 copy-start.2
  0.9 0.9 %copy-done.2 = f32[128,256]{1,0:T(8,128)S(1)} copy-done((f32[128,256]{1,0:T(8,128)S(1)}, f32[128,256]{1,0:T(8,128)}, u32[]{:S(2)}) %copy-start.2) | copy-done | bytes 131096
  1.8 0.0 copy-start.3
  1.8 0.9 %copy-done.3 = f32[128,256]{1,0:T(8,128)S(1)} copy-done((f32[128,256]{1,0:T(8,128)S(1)}, f32[128,256]{1,0:T(8,128)}, u32[]{:S(2)}) %copy-start.3) | copy-done | bytes 131096
  2.7 0.0 copy-start.4
  2.7 0.9 %copy-done.4 = f32[128,256]{1,0:T(8,128)S(1)} copy-done((f32[128,256]{1,0:T(8,128)S(1)}, f32[128,256]{1,0:T(8,128)}, u32[]{:S(2)}) %copy-start.4) | copy-done | bytes 131096
  3.6 0.0 copy-start.5
  3.6 0.9 %copy-done.5 = f32[128,256]{1,0:T(8,128)S(1)} copy-done((f32[128,256]{1,0:T(8,128)S(1)}, f32[128,256]{1,0:T(8,128)}, u32[]{:S(2)}) %copy-start.5) | copy-done | bytes 131096
  4.5 0.0 copy-start.6
  4.5 0.9 %copy-done.6 = f32[128,256]{1,0:T(8,128)S(1)} copy-done((f32[128,256]{1,0:T(8,128)S(1)}, f32[128,256]{1,0:T(8,128)}, u32[]{:S(2)}) %copy-start.6) | copy-done | bytes 131096
  5.4 32.8 %reduce.1 = (f32[8,2048,128]{2,1,0:T(8,128)}, f32[8,8,128]{2,1,0:T(8,128)S(1)}, f32[256,128]{1,0:T(8,128)S(1)}) custom-call(f32[128,64,256]{2,1,0:T(8,128)} %bitcast.2, f32[128,256]{1,0:T(8,128)S(1)} %copy-done.1, f32[128,256]{1,0:T(8,128)S(1)} %copy-done.2, f32[128,256]{1,0:T(8,128)S(1)} %copy-done.3, f32[128,256]{1,0:T(8,128)S(1)} %copy-done.4, ...), custom_call_target="tpu_custom_call" | custom-call | tf_op jit(solution)/shard_map/reduce/pallas_call | solution.py:367
  38.2 0.0 copy-start
  38.2 3.4 %copy-done = f32[8,2048,128]{2,1,0:T(8,128)S(1)} copy-done((f32[8,2048,128]{2,1,0:T(8,128)S(1)}, f32[8,2048,128]{2,1,0:T(8,128)}, u32[]{:S(2)}) %copy-start) | copy-done | bytes 8388632
  41.6 6.2 %finish.1 = f32[128,64,256]{2,1,0:T(8,128)} custom-call(f32[8,2048,128]{2,1,0:T(8,128)S(1)} %copy-done, f32[8,8,128]{2,1,0:T(8,128)S(1)} %get-tuple-element.9.edge_ref, f32[256,128]{1,0:T(8,128)S(1)} %get-tuple-element.10.ratio_ref), custom_call_target="tpu_custom_call" | custom-call | tf_op jit(solution)/shard_map/finish/pallas_call | solution.py:391
Async XLA Ops:
  0.0 0.9 %copy-start.1 = (f32[128,256]{1,0:T(8,128)S(1)}, f32[128,256]{1,0:T(8,128)}, u32[]{:S(2)}) copy-start(f32[128,256]{1,0:T(8,128)} %sub_x.1) | copy-start | bytes 393220
  0.9 0.9 %copy-start.2 = (f32[128,256]{1,0:T(8,128)S(1)}, f32[128,256]{1,0:T(8,128)}, u32[]{:S(2)}) copy-start(f32[128,256]{1,0:T(8,128)} %diag_x.1) | copy-start | bytes 393220
  1.8 0.9 %copy-start.3 = (f32[128,256]{1,0:T(8,128)S(1)}, f32[128,256]{1,0:T(8,128)}, u32[]{:S(2)}) copy-start(f32[128,256]{1,0:T(8,128)} %sup_x.1) | copy-start | bytes 393220
  2.7 0.9 %copy-start.4 = (f32[128,256]{1,0:T(8,128)S(1)}, f32[128,256]{1,0:T(8,128)}, u32[]{:S(2)}) copy-start(f32[128,256]{1,0:T(8,128)} %sub_y.1) | copy-start | bytes 393220
  3.6 0.9 %copy-start.5 = (f32[128,256]{1,0:T(8,128)S(1)}, f32[128,256]{1,0:T(8,128)}, u32[]{:S(2)}) copy-start(f32[128,256]{1,0:T(8,128)} %diag_y.1) | copy-start | bytes 393220
  4.5 0.9 %copy-start.6 = (f32[128,256]{1,0:T(8,128)S(1)}, f32[128,256]{1,0:T(8,128)}, u32[]{:S(2)}) copy-start(f32[128,256]{1,0:T(8,128)} %sup_y.1) | copy-start | bytes 393220
  38.2 3.4 %copy-start = (f32[8,2048,128]{2,1,0:T(8,128)S(1)}, f32[8,2048,128]{2,1,0:T(8,128)}, u32[]{:S(2)}) copy-start(f32[8,2048,128]{2,1,0:T(8,128)} %get-tuple-element.8.g_ref) | copy-start | bytes 25165828

commit v2 on v1

v2 whole, which is shorter than its diff:
```python
import functools

import jax
import jax.numpy as jnp
from jax import lax
from jax.experimental import pallas as pl
from jax.experimental.pallas import tpu as pltpu
from jax.sharding import PartitionSpec as P

MESH = pl.DeviceIdType.MESH
NI, NF, NJ = 128, 64, 256
L, S = 128, 8
FB = NF // S
JB = NJ // L
CH = 4
CB = FB // CH
CV = CB * JB
HR = 8
f32 = jnp.float32
RL, FL = 38_000_000, 6


def bcast(ref, row):
    return jnp.broadcast_to(ref[pl.ds(row, 1), :], (S, L))


def bcast_x(ref, row, jb):
    return jnp.broadcast_to(ref[jb, pl.ds(row, 1), :], (S, L))


HB = FB // 2
HC = CH // 2


def y_eliminate(first_y, g_ref, inv_t, s_t, last_ref, slots):
    U = 8

    def run(ascending):
        def group(t, gs):
            base = pl.multiple_of(t * U if ascending else NJ - U - t * U, U)
            for r in range(U) if ascending else range(U - 1, -1, -1):
                inv, s = bcast(inv_t, base + r), bcast(s_t, base + r)
                rows = pl.ds(base * S + r * S, S)
                new = []
                for fb in range(HB):
                    g = g_ref[fb, rows, :] * inv - s * gs[fb]
                    g_ref[fb, rows, :] = g
                    new.append(g)
                gs = tuple(new)
            return gs

        gs = lax.fori_loop(0, NJ // U, group, tuple(jnp.zeros((S, L), f32) for _ in range(HB)))
        for fb in range(HB):
            last_ref[slots + fb] = gs[fb]

    pl.when(first_y)(lambda: run(True))
    pl.when(jnp.logical_not(first_y))(lambda: run(False))


def y_substitute(first_y, g_ref, ratio_ref, edges):
    U = 8

    def run(ascending):
        def group(t, ws):
            base = pl.multiple_of(t * U if ascending else NJ - U - t * U, U)
            for r in range(U) if ascending else range(U - 1, -1, -1):
                p = bcast(ratio_ref, base + r)
                rows = pl.ds(base * S + r * S, S)
                new = []
                for fb in range(HB):
                    w = g_ref[fb, rows, :] - p * ws[fb]
                    g_ref[fb, rows, :] = w
                    new.append(w)
                ws = tuple(new)
            return ws

        lax.fori_loop(0, NJ // U, group, tuple(edges))

    pl.when(jnp.logical_not(first_y))(lambda: run(True))
    pl.when(first_y)(lambda: run(False))


def to_rows(g_ref, fb, out_ref):
    for jb in range(JB):
        view = out_ref.at[fb * JB + jb].reshape(NI * S, L)
        for f in range(S):
            view[pl.ds(f, NI, stride=S), :] = g_ref[fb, pl.ds(jb * L * S + f, L, stride=S), :].T


def reduce_kernel(u_hbm, sub_x, diag_x, sup_x, sub_y, diag_y, sup_y,
                  done_a, g_b, edge_out, ratio_out,
                  b1, b2, b3, g_a, halo_send, halo_recv,
                  low_x, cen_x, high_x, inv_x, s_x, p_x, f_x, q_x,
                  sy, dy, uy, cen_t, lo_t, hi_t, b_t, a_t, c_t, inv_t, s_t,
                  coef_send, coef_recv, mu_send, mu_recv,
                  fl_send, fl_recv, lam_send, lam_recv, wprev, wnext,
                  yl_send, yl_recv, ymu_send, ymu_recv,
                  cf_sem, in_sem, halo_ss, halo_rs, coef_ss, coef_rs, mu_ss, mu_rs,
                  fl_ss, fl_rs, lam_ss, lam_rs, y_ss, y_rs):
    my_x = lax.axis_index("x")
    my_y = lax.axis_index("y")
    core = lax.rem(my_x, 2)
    chip = my_x // 2
    mate = {"x": my_x + 1 - 2 * core}
    across = {"x": lax.rem(my_x + 2, 4)}
    beside = {"y": 1 - my_y}
    first_core = core == 0
    first_chip = chip == 0
    first_y = my_y == 0

    cf_copies = []
    for src, dst in ((sub_y, sy), (diag_y, dy), (sup_y, uy)):
        cf_copies.append(pltpu.make_async_copy(src, dst, cf_sem.at[len(cf_copies)]))
    for src, dst in ((sub_x, low_x), (diag_x, cen_x), (sup_x, high_x)):
        for jb in range(JB):
            cf_copies.append(pltpu.make_async_copy(
                src.at[:, pl.ds(jb * L, L)], dst.at[jb], cf_sem.at[len(cf_copies)]))
    for copy in cf_copies:
        copy.start()

    def in_copy(fb, jb):
        k = fb * JB + jb
        return pltpu.make_async_copy(
            u_hbm.at[:, pl.ds(fb * S, S), pl.ds(jb * L, L)], b1.at[k], in_sem.at[k])

    for fb in range(FB):
        for jb in range(JB):
            in_copy(fb, jb).start()

    barrier = pltpu.get_barrier_semaphore()
    for peer in (mate, across, beside):
        pl.semaphore_signal(barrier, inc=1, device_id=peer, device_id_type=MESH)

    for copy in cf_copies:
        copy.wait()
    for jb in range(JB):
        cols = slice(jb * L, (jb + 1) * L)
        d = dy[:, cols].T
        lo = sy[:, cols].T
        hi = uy[:, cols].T
        cen_t[cols, :] = 1.0 - d
        b_t[cols, :] = 1.0 + d
        lo_t[cols, :] = lo
        hi_t[cols, :] = hi
        a_t[cols, :] = jnp.where(first_y, lo, hi)
        c_t[cols, :] = jnp.where(first_y, hi, lo)

    def x_factor(row, state):
        out = []
        for jb in range(JB):
            p_prev, f_prev, q, e_sum = state[jb]
            sub, sup = low_x[jb, row, :], high_x[jb, row, :]
            inv = 1.0 / (1.0 + cen_x[jb, row, :] - sub * p_prev)
            p, s = sup * inv, sub * inv
            fill = -s * f_prev
            inv_x[jb, row, :] = inv
            s_x[jb, row, :] = s
            p_x[jb, row, :] = p
            f_x[jb, row, :] = fill
            q_x[jb, row, :] = q
            out.append((p, fill, -q * p, e_sum + q * fill))
        return tuple(out)

    def y_factor(t, p_prev):
        row = pl.ds(jnp.where(first_y, t, NJ - 1 - t), 1)
        low = a_t[row, :]
        inv = 1.0 / (b_t[row, :] - low * p_prev)
        p = c_t[row, :] * inv
        inv_t[row, :] = inv
        s_t[row, :] = low * inv
        ratio_out[row, :] = p
        return p

    pl.semaphore_wait(barrier, 3)

    def halo_copy(fb):
        rows = pl.ds(pl.multiple_of(fb * S, S), S)
        return pltpu.make_async_remote_copy(
            halo_send.at[rows, :], halo_recv.at[rows, :], halo_ss.at[fb], halo_rs.at[fb],
            device_id=beside, device_id_type=MESH)

    def to_columns(fb, state):
        x_state, p = state
        for jb in range(JB):
            in_copy(fb, jb).wait()
        views = [b1.at[fb * JB + jb].reshape(NI * S, L) for jb in range(JB)]
        for f in range(S):
            parts = [views[jb][pl.ds(f, NI, stride=S), :].T for jb in range(JB)]
            for jb in range(JB):
                b2[fb * S + f, HR + jb * L:HR + (jb + 1) * L, :] = parts[jb]
            halo_send[pl.ds(fb * S + f, 1), :] = jnp.where(
                first_y, parts[JB - 1][L - 1:L, :], parts[0][0:1, :])
        for r in range(NI // FB):
            x_state = x_factor(pl.ds(fb * (NI // FB) + r, 1), x_state)
        for r in range(NJ // FB):
            p = y_factor(fb * (NJ // FB) + r, p)
        halo_copy(fb).start()
        return x_state, p

    none = jnp.zeros((1, L), f32)
    ends, p_end = lax.fori_loop(0, FB, to_columns, (((none, none + 1.0, none + 1.0, none),) * JB, none))
    for jb in range(JB):
        p_last, f_last, q_all, e_sum = ends[jb]
        for r, value in enumerate((e_sum, f_last, q_all, -p_last)):
            coef_send[jb, r:r + 1, :] = value
        coef_send[jb, 4:8, :] = jnp.zeros((4, L), f32)
    ymu_send[...] = jnp.broadcast_to(-p_end, (S, L))
    coef_copy = pltpu.make_async_remote_copy(
        coef_send, coef_recv, coef_ss, coef_rs, device_id=mate, device_id_type=MESH)
    ymu_copy = pltpu.make_async_remote_copy(
        ymu_send, ymu_recv, y_ss.at[2], y_rs.at[2], device_id=beside, device_id_type=MESH)

    def stencil(fi, fb):
        f_all = fb * S + fi
        halo = halo_recv[pl.ds(f_all, 1), :]
        none = jnp.zeros_like(halo)
        b2[f_all, HR - 1:HR, :] = jnp.where(first_y, none, halo)
        b2[f_all, HR + NJ:HR + NJ + 1, :] = jnp.where(first_y, halo, none)
        for jb in range(JB):
            base = HR + jb * L
            cols = slice(jb * L, (jb + 1) * L)
            before = b2[f_all, base - 1:base - 1 + L, :]
            here = b2[f_all, base:base + L, :]
            after = b2[f_all, base + 1:base + 1 + L, :]
            r = cen_t[cols, :] * here - lo_t[cols, :] * before - hi_t[cols, :] * after
            b1.at[fb * JB + jb].reshape(NI * S, L)[pl.ds(fi, NI, stride=S), :] = r.T
        return fb

    def fl_copy(c):
        return pltpu.make_async_remote_copy(
            fl_send.at[c], fl_recv.at[c], fl_ss.at[c], fl_rs.at[c], device_id=mate, device_id_type=MESH)

    def lam_copy(c):
        return pltpu.make_async_remote_copy(
            lam_send.at[c], lam_recv.at[c], lam_ss.at[c], lam_rs.at[c], device_id=across, device_id_type=MESH)

    mu_copy = pltpu.make_async_remote_copy(
        mu_send, mu_recv, mu_ss, mu_rs, device_id=across, device_id_type=MESH)

    def x_forward(c):
        U = 8

        def group(t, state):
            base = pl.multiple_of(t * U, U)
            gs, accs = state
            for r in range(U):
                inv = [bcast_x(inv_x, base + r, jb) for jb in range(JB)]
                s = [bcast_x(s_x, base + r, jb) for jb in range(JB)]
                q = [bcast_x(q_x, base + r, jb) for jb in range(JB)]
                new_g, new_acc = [], []
                for v in range(CV):
                    jb = v % JB
                    g = b1[c * CV + v, base + r] * inv[jb] - s[jb] * gs[v]
                    b3[c * CV + v, base + r] = g
                    new_g.append(g)
                    new_acc.append(accs[v] + q[jb] * g)
                gs, accs = tuple(new_g), tuple(new_acc)
            return gs, accs

        zeros = tuple(jnp.zeros((S, L), f32) for _ in range(CV))
        gs, accs = lax.fori_loop(0, NI // U, group, (zeros, zeros))
        for v in range(CV):
            fl_send[c, 0, v] = accs[v]
            fl_send[c, 1, v] = gs[v]
        fl_copy(c).start()

    def pair_coefs(jb):
        def both(row):
            mine, other = coef_send[jb, row:row + 1, :], coef_recv[jb, row:row + 1, :]
            return jnp.where(first_core, mine, other), jnp.where(first_core, other, mine)

        ef, el, qf, ql = both(0), both(1), both(2), both(3)
        return ef, el, qf, ql, 1.0 / (1.0 - ql[0] * ef[1])

    def own_mu(jb):
        ef, el, qf, ql, det = pair_coefs(jb)
        return jnp.where(first_chip, el[1] * det * ql[0] * qf[1] + ql[1], ef[0] + qf[0] * ef[1] * det * el[0])

    def up(row):
        return jnp.broadcast_to(row, (S, L))

    def pair_data(c, v):
        f_mine, f_other = fl_send[c, 0, v], fl_recv[c, 0, v]
        l_mine, l_other = fl_send[c, 1, v], fl_recv[c, 1, v]
        f0, f1 = jnp.where(first_core, f_mine, f_other), jnp.where(first_core, f_other, f_mine)
        l0, l1 = jnp.where(first_core, l_mine, l_other), jnp.where(first_core, l_other, l_mine)
        return f0, f1, l0, l1

    def merge(c):
        fl_copy(c).wait_recv()
        for v in range(CV):
            ef, el, qf, ql, det = pair_coefs(v % JB)
            f0, f1, l0, l1 = pair_data(c, v)
            last0 = up(det) * (l0 + up(ql[0]) * f1)
            first1 = f1 + up(ef[1]) * last0
            lam_send[c, v] = jnp.where(first_chip, l1 + up(el[1]) * last0, f0 + up(qf[0]) * first1)
        lam_copy(c).start()

    def settle(c):
        lam_copy(c).wait_recv()
        for v in range(CV):
            jb = v % JB
            ef, el, qf, ql, det = pair_coefs(jb)
            f0, f1, l0, l1 = pair_data(c, v)
            mu_mine, mu_other = mu_send[jb], mu_recv[jb]
            mid = (lam_recv[c, v] + mu_other * lam_send[c, v]) / (1.0 - mu_mine * mu_other)
            zero = jnp.zeros_like(mid)
            prev, nxt = jnp.where(first_chip, zero, mid), jnp.where(first_chip, mid, zero)
            rest = f1 + up(qf[1]) * nxt
            last0 = up(det) * (l0 + up(el[0]) * prev + up(ql[0]) * rest)
            first1 = rest + up(ef[1]) * last0
            wprev[c, v] = jnp.where(first_core, prev, last0)
            wnext[c, v] = jnp.where(first_core, first1, nxt)

    def x_backward(c):
        U = 8
        prevs = [wprev[c, v] for v in range(CV)]

        def group(t, ws):
            base = pl.multiple_of(NI - U - t * U, U)
            for r in range(U - 1, -1, -1):
                fill = [bcast_x(f_x, base + r, jb) for jb in range(JB)]
                p = [bcast_x(p_x, base + r, jb) for jb in range(JB)]
                new = []
                for v in range(CV):
                    jb = v % JB
                    w = b3[c * CV + v, base + r] + fill[jb] * prevs[v] - p[jb] * ws[v]
                    b1[c * CV + v, base + r] = w + (w - b1[c * CV + v, base + r])
                    new.append(w)
                ws = tuple(new)
            return ws

        lax.fori_loop(0, NI // U, group, tuple(wnext[c, v] for v in range(CV)))

    def turn(fb, g_ref, slot):
        for jb in range(JB):
            view = b1.at[fb * JB + jb].reshape(NI * S, L)
            for f in range(S):
                g_ref[slot, pl.ds(jb * L * S + f, L, stride=S), :] = view[pl.ds(f, NI, stride=S), :].T

    def y_copy(half):
        rows = pl.ds(half * HB, HB)
        return pltpu.make_async_remote_copy(
            yl_send.at[rows], yl_recv.at[rows], y_ss.at[half], y_rs.at[half],
            device_id=beside, device_id_type=MESH)

    def y_edges(half):
        y_copy(half).wait_recv()
        mu_mine, mu_other = ymu_send[...], ymu_recv[...]
        scale = 1.0 / (1.0 - mu_mine * mu_other)
        return [(yl_recv[half * HB + fb] + mu_other * yl_send[half * HB + fb]) * scale for fb in range(HB)]

    for c in range(CH):
        for fb in range(c * CB, (c + 1) * CB):
            halo_copy(fb).wait_recv()
            lax.fori_loop(0, S, stencil, fb, unroll=4)
        if c == 0:
            coef_copy.start()
            ymu_copy.start()
        x_forward(c)
        if c == 0:
            coef_copy.wait_recv()
            for jb in range(JB):
                mu_send[jb] = up(own_mu(jb))
        else:
            if c == 1:
                mu_copy.start()
            merge(c - 1)
    mu_copy.wait_recv()
    for c in range(CH):
        settle(c)
        x_backward(c)
        if c == 0:
            merge(CH - 1)
        for fb in range(c * CB, (c + 1) * CB):
            turn(fb, g_a if c < HC else g_b, fb % HB)
        if c == HC - 1:
            y_eliminate(first_y, g_a, inv_t, s_t, yl_send, 0)
            y_copy(0).start()
    y_eliminate(first_y, g_b, inv_t, s_t, yl_send, HB)
    y_copy(1).start()
    ymu_copy.wait_recv()
    y_substitute(first_y, g_a, ratio_out, y_edges(0))
    for fb in range(HB):
        to_rows(g_a, fb, done_a)
    for fb, value in enumerate(y_edges(1)):
        edge_out[fb] = value

    ymu_copy.wait_send()
    coef_copy.wait_send()
    mu_copy.wait_send()
    for half in range(2):
        y_copy(half).wait_send()
    for fb in range(FB):
        halo_copy(fb).wait_send()
    for c in range(CH):
        fl_copy(c).wait_send()
        lam_copy(c).wait_send()


def finish_kernel(done_a, g_ref, edge_ref, ratio_ref, out_hbm, buf, out_sem):
    first_y = lax.axis_index("y") == 0

    def out_copy(ref, fb, jb, first):
        k = fb * JB + jb
        return pltpu.make_async_copy(
            ref.at[k], out_hbm.at[:, pl.ds((first + fb) * S, S), pl.ds(jb * L, L)],
            out_sem.at[first * JB + k])

    for fb in range(HB):
        for jb in range(JB):
            out_copy(done_a, fb, jb, 0).start()
    y_substitute(first_y, g_ref, ratio_ref, [edge_ref[fb] for fb in range(HB)])
    for fb in range(HB):
        to_rows(g_ref, fb, buf)
        for jb in range(JB):
            out_copy(buf, fb, jb, HB).start()
    for fb in range(HB):
        for jb in range(JB):
            out_copy(done_a, fb, jb, 0).wait()
            out_copy(buf, fb, jb, HB).wait()


def solution(mesh):
    tile_spec = P(("batch", "x"), "y", None)
    coef_spec = P(("batch", "x"), "y")
    vmem = pl.BlockSpec(memory_space=pltpu.VMEM)
    hbm = pl.BlockSpec(memory_space=pltpu.HBM)
    V, DMA = pltpu.VMEM, pltpu.SemaphoreType.DMA
    row_x, col_t = V((JB, NI, L), f32), V((NJ, NI), f32)

    def local_step(field, *coefs):
        done, g, edge, ratio = pl.pallas_call(
            reduce_kernel,
            out_shape=(jax.ShapeDtypeStruct((HB * JB, NI, S, L), f32),
                       jax.ShapeDtypeStruct((HB, NJ * S, L), f32),
                       jax.ShapeDtypeStruct((HB, S, L), f32),
                       jax.ShapeDtypeStruct((NJ, L), f32)),
            in_specs=[hbm] * 7,
            out_specs=(vmem, vmem, vmem, vmem),
            scratch_shapes=[
                V((FB * JB, NI, S, L), f32), V((NF, NJ + 2 * HR, L), f32), V((FB * JB, NI, S, L), f32),
                V((HB, NJ * S, L), f32),
                V((NF, L), f32), V((NF, L), f32),
                row_x, row_x, row_x, row_x, row_x, row_x, row_x, row_x,
                V((NI, NJ), f32), V((NI, NJ), f32), V((NI, NJ), f32),
                col_t, col_t, col_t, col_t, col_t, col_t, col_t, col_t,
                V((JB, S, L), f32), V((JB, S, L), f32), V((JB, S, L), f32), V((JB, S, L), f32),
                V((CH, 2, CV, S, L), f32), V((CH, 2, CV, S, L), f32),
                V((CH, CV, S, L), f32), V((CH, CV, S, L), f32),
                V((CH, CV, S, L), f32), V((CH, CV, S, L), f32),
                V((FB, S, L), f32), V((FB, S, L), f32), V((S, L), f32), V((S, L), f32),
                DMA((9,)), DMA((FB * JB,)), DMA((FB,)), DMA((FB,)), DMA, DMA, DMA, DMA,
                DMA((CH,)), DMA((CH,)), DMA((CH,)), DMA((CH,)), DMA((3,)), DMA((3,)),
            ],
            compiler_params=pltpu.CompilerParams(
                collective_id=0, has_side_effects=True, vmem_limit_bytes=RL),
            name="reduce",
        )(*(pltpu.with_memory_space_constraint(x, pltpu.HBM) for x in (jnp.swapaxes(field, 1, 2), *coefs)))
        out = pl.pallas_call(
            finish_kernel,
            out_shape=jax.ShapeDtypeStruct((NI, NF, NJ), f32),
            in_specs=[vmem] * 4,
            out_specs=hbm,
            scratch_shapes=[V((HB * JB, NI, S, L), f32), DMA((FB * JB,))],
            compiler_params=pltpu.CompilerParams(vmem_limit_bytes=FL << 20),
            name="finish",
        )(done, g, edge, ratio)
        return jnp.swapaxes(out, 1, 2)

    return jax.shard_map(local_step, mesh=mesh, in_specs=(tile_spec,) + (coef_spec,) * 6,
                         out_specs=tile_spec, check_vma=False)
```

time: 48 us -> 28.8 us (0.60)
  Pallas kernels: 39 us -> 28.7 us
  local copies, waits for them, and re-layouts: 8.8 us -> 0 us
    unnamed x14 -> x0, local copies, waits for them, and re-layouts: 8.8 us -> none
    pallas_call x1, Pallas kernels: 32.8 us -> 25.3 us  [local_step(): pl.pallas_call(reduce_kernel, out_shape=(jax.ShapeDtypeStruct((HB * JB, N...]
    pallas_call x1, Pallas kernels: 6.21 us -> 3.42 us  [local_step(): pl.pallas_call(finish_kernel, out_shape=jax.ShapeDtypeStruct((NI, NF, NJ)...]
where the time goes in v2:
time: 28.8 us
  Pallas kernels  28.7 us (100%)
    pallas_call x1, Pallas kernels, local_step(): pl.pallas_call(reduce_kernel, out_shape=(jax.ShapeDtypeStruct((HB * JB, N...  25.3 us
    pallas_call x1, Pallas kernels, local_step(): pl.pallas_call(finish_kernel, out_shape=jax.ShapeDtypeStruct((NI, NF, NJ)...  3.42 us

profile of v2, /device:TPU:0, one launch (start us, length us, event | category | flops | bytes accessed | tf_op | source)
XLA Modules:
  0.0 28.8 jit_solution(1608724357274199696)
XLA Ops:
  0.0 25.3 %reduce.1 = (f32[8,128,8,128]{3,2,1,0:T(8,128)S(1)}, f32[4,2048,128]{2,1,0:T(8,128)S(1)}, f32[4,8,128]{2,1,0:T(8,128)S(1)}, f32[256,128]{1,0:T(8,128)S(1)}) custom-call(f32[128,64,256]{2,1,0:T(8,128)} %bitcast.2, f32[128,256]{1,0:T(8,128)} %sub_x.1, f32[128,256]{1,0:T(8,128)} %diag_x.1, f32[128,256]{1,0:T(8,128)} %sup_x.1, f32[128,256]{1,0:T(8,128)} %sub_y.1, ...), custom_call_target="tpu_custom_call" | custom-call | tf_op jit(solution)/shard_map/reduce/pallas_call | solution.py:433
  25.3 3.4 %finish.1 = f32[128,64,256]{2,1,0:T(8,128)} custom-call(f32[8,128,8,128]{3,2,1,0:T(8,128)S(1)} %get-tuple-element.9.done_a, f32[4,2048,128]{2,1,0:T(8,128)S(1)} %get-tuple-element.10.g_ref, f32[4,8,128]{2,1,0:T(8,128)S(1)} %get-tuple-element.11.edge_ref, f32[256,128]{1,0:T(8,128)S(1)} %get-tuple-element.12.ratio_ref), custom_call_target="tpu_custom_call" | custom-call | tf_op jit(solution)/shard_map/finish/pallas_call | solution.py:460

commit v3 on v2

v3 whole, which is shorter than its diff:
```python
import functools

import jax
import jax.numpy as jnp
from jax import lax
from jax.experimental import pallas as pl
from jax.experimental.pallas import tpu as pltpu
from jax.sharding import PartitionSpec as P

MESH = pl.DeviceIdType.MESH
NI, NF, NJ = 128, 64, 256
L, S = 128, 8
FB = NF // S
JB = NJ // L
CH = 4
CB = FB // CH
CV = CB * JB
HR = 8
f32 = jnp.float32
RL, FL = 44_000_000, 6


def spelled(n, body, state):
    return lax.fori_loop(0, n, body, state, unroll=True)


def aligned(i):
    return pl.multiple_of(i, S)


def bcast(ref, row):
    return jnp.broadcast_to(ref[pl.ds(row, 1), :], (HB, S, L))


def bcast_x(ref, row):
    return jnp.broadcast_to(ref[:, pl.ds(row, 1), :], (CB, JB, S, L))


HB = FB // 2
HC = CH // 2


def y_eliminate(first_y, g_ref, inv_t, s_t, last_ref, slots):
    U = 8

    def run(ascending):
        def group(t, gs):
            base = pl.multiple_of(t * U if ascending else NJ - U - t * U, U)

            def row(r, gs):
                j = base + (r if ascending else U - 1 - r)
                rows = pl.ds(aligned(j * S), S)
                gs = g_ref[:, rows, :] * bcast(inv_t, j) - bcast(s_t, j) * gs
                g_ref[:, rows, :] = gs
                return gs

            return spelled(U, row, gs)

        last_ref[slots:slots + HB] = lax.fori_loop(0, NJ // U, group, jnp.zeros((HB, S, L), f32))

    pl.when(first_y)(lambda: run(True))
    pl.when(jnp.logical_not(first_y))(lambda: run(False))


def y_substitute(first_y, g_ref, ratio_ref, edges):
    U = 8

    def run(ascending):
        def group(t, ws):
            base = pl.multiple_of(t * U if ascending else NJ - U - t * U, U)

            def row(r, ws):
                j = base + (r if ascending else U - 1 - r)
                rows = pl.ds(aligned(j * S), S)
                ws = g_ref[:, rows, :] - bcast(ratio_ref, j) * ws
                g_ref[:, rows, :] = ws
                return ws

            return spelled(U, row, ws)

        lax.fori_loop(0, NJ // U, group, edges)

    pl.when(jnp.logical_not(first_y))(lambda: run(True))
    pl.when(first_y)(lambda: run(False))


def to_rows(g_ref, fb, out_ref, after=None):
    for jb in range(JB):
        view = out_ref.at[fb * JB + jb].reshape(NI * S, L)

        def one(f, _):
            view[pl.ds(f, NI, stride=S), :] = g_ref[fb, pl.ds(jb * L * S + f, L, stride=S), :].T
            return 0

        spelled(S, one, 0)
        if after is not None:
            after(jb)


def reduce_kernel(u_hbm, sub_x, diag_x, sup_x, sub_y, diag_y, sup_y,
                  done_a, g_b, edge_out, ratio_out,
                  u_in, b1s, b2, b3s, g_a, halo_send, halo_recv,
                  low_x, cen_x, high_x, inv_x, s_x, p_x, f_x, q_x,
                  sy, dy, uy, cen_t, lo_t, hi_t, b_t, a_t, c_t, inv_t, s_t,
                  coef_send, coef_recv, mu_send, mu_recv,
                  fl_send, fl_recv, lam_send, lam_recv, wprev, wnext,
                  yl_send, yl_recv, ymu_send, ymu_recv,
                  cf_sem, in_sem, halo_ss, halo_rs, coef_ss, coef_rs, mu_ss, mu_rs,
                  fl_ss, fl_rs, lam_ss, lam_rs, y_ss, y_rs):
    my_x = lax.axis_index("x")
    my_y = lax.axis_index("y")
    core = lax.rem(my_x, 2)
    chip = my_x // 2
    mate = {"x": my_x + 1 - 2 * core}
    across = {"x": lax.rem(my_x + 2, 4)}
    beside = {"y": 1 - my_y}
    first_core = core == 0
    first_chip = chip == 0
    first_y = my_y == 0

    cf_copies = []
    for src, dst in ((sub_y, sy), (diag_y, dy), (sup_y, uy)):
        cf_copies.append(pltpu.make_async_copy(src, dst, cf_sem.at[len(cf_copies)]))
    for src, dst in ((sub_x, low_x), (diag_x, cen_x), (sup_x, high_x)):
        for jb in range(JB):
            cf_copies.append(pltpu.make_async_copy(
                src.at[:, pl.ds(jb * L, L)], dst.at[jb], cf_sem.at[len(cf_copies)]))
    for copy in cf_copies:
        copy.start()

    def in_copy(fb, jb):
        return pltpu.make_async_copy(
            u_hbm.at[:, pl.ds(aligned(fb * S), S), pl.ds(jb * L, L)],
            u_in.at[fb, jb], in_sem.at[fb * JB + jb])

    def start_in(fb, _):
        for jb in range(JB):
            in_copy(fb, jb).start()
        return 0

    lax.fori_loop(0, FB, start_in, 0)

    barrier = pltpu.get_barrier_semaphore()
    for peer in (mate, across, beside):
        pl.semaphore_signal(barrier, inc=1, device_id=peer, device_id_type=MESH)

    for copy in cf_copies:
        copy.wait()
    for jb in range(JB):
        cols = slice(jb * L, (jb + 1) * L)
        d = dy[:, cols].T
        lo = sy[:, cols].T
        hi = uy[:, cols].T
        cen_t[cols, :] = 1.0 - d
        b_t[cols, :] = 1.0 + d
        lo_t[cols, :] = lo
        hi_t[cols, :] = hi
        a_t[cols, :] = jnp.where(first_y, lo, hi)
        c_t[cols, :] = jnp.where(first_y, hi, lo)

    def x_factor(i, state):
        row = pl.ds(i, 1)
        p_prev, f_prev, q, e_sum = state
        sub, sup = low_x[:, row, :], high_x[:, row, :]
        inv = 1.0 / (1.0 + cen_x[:, row, :] - sub * p_prev)
        p, s = sup * inv, sub * inv
        fill = -s * f_prev
        inv_x[:, row, :] = inv
        s_x[:, row, :] = s
        p_x[:, row, :] = p
        f_x[:, row, :] = fill
        q_x[:, row, :] = q
        return p, fill, -q * p, e_sum + q * fill

    def y_factor(t, p_prev):
        row = pl.ds(jnp.where(first_y, t, NJ - 1 - t), 1)
        low = a_t[row, :]
        inv = 1.0 / (b_t[row, :] - low * p_prev)
        p = c_t[row, :] * inv
        inv_t[row, :] = inv
        s_t[row, :] = low * inv
        ratio_out[row, :] = p
        return p

    pl.semaphore_wait(barrier, 3)

    def halo_copy(fb):
        rows = pl.ds(pl.multiple_of(fb * S, S), S)
        return pltpu.make_async_remote_copy(
            halo_send.at[rows, :], halo_recv.at[rows, :], halo_ss.at[fb], halo_rs.at[fb],
            device_id=beside, device_id_type=MESH)

    def to_columns(fb, state):
        x_state, p = state
        for jb in range(JB):
            in_copy(fb, jb).wait()
        views = [u_in.at[fb, jb].reshape(NI * S, L) for jb in range(JB)]

        def one(f, _):
            parts = [views[jb][pl.ds(f, NI, stride=S), :].T for jb in range(JB)]
            for jb in range(JB):
                b2[fb * S + f, HR + jb * L:HR + (jb + 1) * L, :] = parts[jb]
            halo_send[pl.ds(fb * S + f, 1), :] = jnp.where(
                first_y, parts[JB - 1][L - 1:L, :], parts[0][0:1, :])
            return 0

        spelled(S, one, 0)
        x_state = spelled(NI // FB, lambda r, st: x_factor(fb * (NI // FB) + r, st), x_state)
        p = spelled(NJ // FB, lambda r, q: y_factor(fb * (NJ // FB) + r, q), p)
        halo_copy(fb).start()
        return x_state, p

    none = jnp.zeros((JB, 1, L), f32)
    (p_last, f_last, q_all, e_sum), p_end = lax.fori_loop(
        0, FB, to_columns, ((none, none + 1.0, none + 1.0, none), none[0]))
    for r, value in enumerate((e_sum, f_last, q_all, -p_last)):
        coef_send[:, r:r + 1, :] = value
    coef_send[:, 4:8, :] = jnp.zeros((JB, 4, L), f32)
    ymu_send[...] = jnp.broadcast_to(-p_end, (S, L))
    coef_copy = pltpu.make_async_remote_copy(
        coef_send, coef_recv, coef_ss, coef_rs, device_id=mate, device_id_type=MESH)
    ymu_copy = pltpu.make_async_remote_copy(
        ymu_send, ymu_recv, y_ss.at[2], y_rs.at[2], device_id=beside, device_id_type=MESH)

    def set_halo(fb):
        def one(f, _):
            halo = halo_recv[pl.ds(fb * S + f, 1), :]
            none = jnp.zeros_like(halo)
            b2[fb * S + f, HR - 1:HR, :] = jnp.where(first_y, none, halo)
            b2[fb * S + f, HR + NJ:HR + NJ + 1, :] = jnp.where(first_y, halo, none)
            return 0

        spelled(S, one, 0)

    def stencil(c, h, fs, jb):
        cols = slice(jb * L, (jb + 1) * L)
        at = HR + jb * L
        cen, lo, hi = cen_t[cols, :], lo_t[cols, :], hi_t[cols, :]
        for f in fs:
            f_all = (c * CB + h) * S + f
            r = (cen * b2[f_all, at:at + L, :] - lo * b2[f_all, at - 1:at - 1 + L, :]
                 - hi * b2[f_all, at + 1:at + 1 + L, :])
            b1s[c].at[h, jb].reshape(NI * S, L)[pl.ds(f, NI, stride=S), :] = r.T

    def fl_copy(c):
        return pltpu.make_async_remote_copy(
            fl_send.at[c], fl_recv.at[c], fl_ss.at[c], fl_rs.at[c], device_id=mate, device_id_type=MESH)

    def lam_copy(c):
        return pltpu.make_async_remote_copy(
            lam_send.at[c], lam_recv.at[c], lam_ss.at[c], lam_rs.at[c], device_id=across, device_id_type=MESH)

    mu_copy = pltpu.make_async_remote_copy(
        mu_send, mu_recv, mu_ss, mu_rs, device_id=across, device_id_type=MESH)

    def x_forward_rows(c, base, n, state):
        def row(r, state):
            i = base + r
            g, acc = state
            g = b1s[c][:, :, i] * bcast_x(inv_x, i) - bcast_x(s_x, i) * g
            b3s[c][:, :, i] = g
            return g, acc + bcast_x(q_x, i) * g

        return spelled(n, row, state)

    def forward_stage(c, nxt):
        if nxt is not None:
            for h in range(CB):
                halo_copy(nxt * CB + h).wait_recv()

        def half(h, state):
            if nxt is not None:
                set_halo(nxt * CB + h)
            span = NI // CB
            parts = S // 2 * JB
            n = span // parts

            def part(k, state):
                for jb in range(JB):
                    if nxt is not None:
                        stencil(nxt, h, (2 * k, 2 * k + 1), jb)
                    if c is not None:
                        state = x_forward_rows(c, h * span + (k * JB + jb) * n, n, state)
                return state

            return spelled(S // 2, part, state)

        zeros = jnp.zeros((CB, JB, S, L), f32)
        g, acc = lax.fori_loop(0, CB, half, (zeros, zeros))
        if c is not None:
            fl_send[c, 0] = acc
            fl_send[c, 1] = g
            fl_copy(c).start()

    def pair_coefs():
        def both(row):
            mine, other = coef_send[:, row:row + 1, :], coef_recv[:, row:row + 1, :]
            return jnp.where(first_core, mine, other), jnp.where(first_core, other, mine)

        ef, el, qf, ql = both(0), both(1), both(2), both(3)
        return ef, el, qf, ql, 1.0 / (1.0 - ql[0] * ef[1])

    def own_mu():
        ef, el, qf, ql, det = pair_coefs()
        return jnp.where(first_chip, el[1] * det * ql[0] * qf[1] + ql[1], ef[0] + qf[0] * ef[1] * det * el[0])

    def up(rows):
        return jnp.broadcast_to(rows, (CB, JB, S, L))

    def pair_data(c):
        f_mine, f_other = fl_send[c, 0], fl_recv[c, 0]
        l_mine, l_other = fl_send[c, 1], fl_recv[c, 1]
        f0, f1 = jnp.where(first_core, f_mine, f_other), jnp.where(first_core, f_other, f_mine)
        l0, l1 = jnp.where(first_core, l_mine, l_other), jnp.where(first_core, l_other, l_mine)
        return f0, f1, l0, l1

    def merge(c):
        fl_copy(c).wait_recv()
        ef, el, qf, ql, det = pair_coefs()
        f0, f1, l0, l1 = pair_data(c)
        last0 = up(det) * (l0 + up(ql[0]) * f1)
        first1 = f1 + up(ef[1]) * last0
        lam_send[c] = jnp.where(first_chip, l1 + up(el[1]) * last0, f0 + up(qf[0]) * first1)
        lam_copy(c).start()

    def settle(c):
        lam_copy(c).wait_recv()
        ef, el, qf, ql, det = pair_coefs()
        f0, f1, l0, l1 = pair_data(c)
        mu_mine, mu_other = mu_send[...], mu_recv[...]
        scale = 1.0 / (1.0 - mu_mine * mu_other)
        mid = (lam_recv[c] + mu_other[None] * lam_send[c]) * scale[None]
        zero = jnp.zeros_like(mid)
        prev, nxt = jnp.where(first_chip, zero, mid), jnp.where(first_chip, mid, zero)
        rest = f1 + up(qf[1]) * nxt
        last0 = up(det) * (l0 + up(el[0]) * prev + up(ql[0]) * rest)
        first1 = rest + up(ef[1]) * last0
        wprev[c] = jnp.where(first_core, prev, last0)
        wnext[c] = jnp.where(first_core, first1, nxt)

    def x_backward_rows(c, base, n, prev, w):
        def row(r, w):
            i = base + (n - 1 - r)
            w = b3s[c][:, :, i] + bcast_x(f_x, i) * prev - bcast_x(p_x, i) * w
            b1s[c][:, :, i] = w + (w - b1s[c][:, :, i])
            return w

        return spelled(n, row, w)

    def backward_stage(c, prior):
        prevs = wprev[c] if c is not None else None

        def half(h, ws):
            span = NI // CB

            def part(f, ws):
                if c is not None:
                    ws = x_backward_rows(c, (CB - 1 - h) * span + (S - 1 - f) * (span // S), span // S, prevs, ws)
                if prior is not None:
                    g_ref = g_a if prior < HC else g_b
                    for jb in range(JB):
                        view = b1s[prior].at[h, jb].reshape(NI * S, L)
                        g_ref[(prior % HC) * CB + h, pl.ds(jb * L * S + f, L, stride=S), :] = (
                            view[pl.ds(f, NI, stride=S), :].T)
                return ws

            return spelled(S, part, ws)

        start = wnext[c] if c is not None else 0
        lax.fori_loop(0, CB, half, start)

    def y_copy(half):
        rows = pl.ds(half * HB, HB)
        return pltpu.make_async_remote_copy(
            yl_send.at[rows], yl_recv.at[rows], y_ss.at[half], y_rs.at[half],
            device_id=beside, device_id_type=MESH)

    def y_edges(half):
        y_copy(half).wait_recv()
        mu_mine, mu_other = ymu_send[...], ymu_recv[...]
        scale = 1.0 / (1.0 - mu_mine * mu_other)
        rows = slice(half * HB, (half + 1) * HB)
        return (yl_recv[rows] + mu_other * yl_send[rows]) * scale

    coef_copy.start()
    ymu_copy.start()
    forward_stage(None, 0)
    forward_stage(0, 1)
    coef_copy.wait_recv()
    mu_send[...] = jnp.broadcast_to(own_mu(), (JB, S, L))
    for c in range(1, CH):
        forward_stage(c, c + 1 if c + 1 < CH else None)
        if c == 1:
            mu_copy.start()
        merge(c - 1)
    mu_copy.wait_recv()
    settle(0)
    backward_stage(0, None)
    merge(CH - 1)
    for c in range(1, CH):
        if c == HC + 1:
            y_eliminate(first_y, g_a, inv_t, s_t, yl_send, 0)
            y_copy(0).start()
        settle(c)
        backward_stage(c, c - 1)
    backward_stage(None, CH - 1)
    y_eliminate(first_y, g_b, inv_t, s_t, yl_send, HB)
    y_copy(1).start()
    ymu_copy.wait_recv()
    y_substitute(first_y, g_a, ratio_out, y_edges(0))
    for fb in range(HB):
        to_rows(g_a, fb, done_a)
    edge_out[...] = y_edges(1)

    ymu_copy.wait_send()
    coef_copy.wait_send()
    mu_copy.wait_send()
    for half in range(2):
        y_copy(half).wait_send()
    for fb in range(FB):
        halo_copy(fb).wait_send()
    for c in range(CH):
        fl_copy(c).wait_send()
        lam_copy(c).wait_send()


def finish_kernel(done_a, g_ref, edge_ref, ratio_ref, out_hbm, buf, out_sem):
    first_y = lax.axis_index("y") == 0

    def out_copy(ref, fb, jb, first):
        k = fb * JB + jb
        return pltpu.make_async_copy(
            ref.at[k], out_hbm.at[:, pl.ds((first + fb) * S, S), pl.ds(jb * L, L)],
            out_sem.at[first * JB + k])

    for fb in range(HB):
        for jb in range(JB):
            out_copy(done_a, fb, jb, 0).start()
    y_substitute(first_y, g_ref, ratio_ref, edge_ref[...])
    for fb in range(HB):
        to_rows(g_ref, fb, buf, lambda jb, fb=fb: out_copy(buf, fb, jb, HB).start())
    for fb in range(HB):
        for jb in range(JB):
            out_copy(done_a, fb, jb, 0).wait()
            out_copy(buf, fb, jb, HB).wait()


def solution(mesh):
    tile_spec = P(("batch", "x"), "y", None)
    coef_spec = P(("batch", "x"), "y")
    vmem = pl.BlockSpec(memory_space=pltpu.VMEM)
    hbm = pl.BlockSpec(memory_space=pltpu.HBM)
    V, DMA = pltpu.VMEM, pltpu.SemaphoreType.DMA
    row_x, col_t = V((JB, NI, L), f32), V((NJ, NI), f32)

    def local_step(field, *coefs):
        done, g, edge, ratio = pl.pallas_call(
            reduce_kernel,
            out_shape=(jax.ShapeDtypeStruct((HB * JB, NI, S, L), f32),
                       jax.ShapeDtypeStruct((HB, NJ * S, L), f32),
                       jax.ShapeDtypeStruct((HB, S, L), f32),
                       jax.ShapeDtypeStruct((NJ, L), f32)),
            in_specs=[hbm] * 7,
            out_specs=(vmem, vmem, vmem, vmem),
            scratch_shapes=[
                V((FB, JB, NI, S, L), f32), [V((CB, JB, NI, S, L), f32)] * CH, V((NF, NJ + 2 * HR, L), f32), [V((CB, JB, NI, S, L), f32)] * CH,
                V((HB, NJ * S, L), f32),
                V((NF, L), f32), V((NF, L), f32),
                row_x, row_x, row_x, row_x, row_x, row_x, row_x, row_x,
                V((NI, NJ), f32), V((NI, NJ), f32), V((NI, NJ), f32),
                col_t, col_t, col_t, col_t, col_t, col_t, col_t, col_t,
                V((JB, S, L), f32), V((JB, S, L), f32), V((JB, S, L), f32), V((JB, S, L), f32),
                V((CH, 2, CB, JB, S, L), f32), V((CH, 2, CB, JB, S, L), f32),
                V((CH, CB, JB, S, L), f32), V((CH, CB, JB, S, L), f32),
                V((CH, CB, JB, S, L), f32), V((CH, CB, JB, S, L), f32),
                V((FB, S, L), f32), V((FB, S, L), f32), V((S, L), f32), V((S, L), f32),
                DMA((9,)), DMA((FB * JB,)), DMA((FB,)), DMA((FB,)), DMA, DMA, DMA, DMA,
                DMA((CH,)), DMA((CH,)), DMA((CH,)), DMA((CH,)), DMA((3,)), DMA((3,)),
            ],
            compiler_params=pltpu.CompilerParams(
                collective_id=0, has_side_effects=True, vmem_limit_bytes=RL),
            name="reduce",
        )(*(pltpu.with_memory_space_constraint(x, pltpu.HBM) for x in (jnp.swapaxes(field, 1, 2), *coefs)))
        out = pl.pallas_call(
            finish_kernel,
            out_shape=jax.ShapeDtypeStruct((NI, NF, NJ), f32),
            in_specs=[vmem] * 4,
            out_specs=hbm,
            scratch_shapes=[V((HB * JB, NI, S, L), f32), DMA((FB * JB,))],
            compiler_params=pltpu.CompilerParams(vmem_limit_bytes=FL << 20),
            name="finish",
        )(done, g, edge, ratio)
        return jnp.swapaxes(out, 1, 2)

    return jax.shard_map(local_step, mesh=mesh, in_specs=(tile_spec,) + (coef_spec,) * 6,
                         out_specs=tile_spec, check_vma=False)
```

time: 28.8 us -> 26.7 us (0.927)
  Pallas kernels: 28.7 us -> 26.6 us
    pallas_call x1, Pallas kernels: 25.3 us -> 23.2 us  [local_step(): pl.pallas_call(reduce_kernel, out_shape=(jax.ShapeDtypeStruct((HB * JB, N...]
where the time goes in v3:
time: 26.7 us; the launch traced here: 26.6 us
  Pallas kernels  26.6 us (100%)
    pallas_call x1, Pallas kernels, local_step(): pl.pallas_call(reduce_kernel, out_shape=(jax.ShapeDtypeStruct((HB * JB, N...  23.2 us
    pallas_call x1, Pallas kernels, local_step(): pl.pallas_call(finish_kernel, out_shape=jax.ShapeDtypeStruct((NI, NF, NJ)...  3.42 us

profile of v3, /device:TPU:0, one launch (start us, length us, event | category | flops | bytes accessed | tf_op | source)
XLA Modules:
  0.0 26.6 jit_solution(5409495994311452822)
XLA Ops:
  0.0 23.2 %reduce.1 = (f32[8,128,8,128]{3,2,1,0:T(8,128)S(1)}, f32[4,2048,128]{2,1,0:T(8,128)S(1)}, f32[4,8,128]{2,1,0:T(8,128)S(1)}, f32[256,128]{1,0:T(8,128)S(1)}) custom-call(f32[128,64,256]{2,1,0:T(8,128)} %bitcast.2, f32[128,256]{1,0:T(8,128)} %sub_x.1, f32[128,256]{1,0:T(8,128)} %diag_x.1, f32[128,256]{1,0:T(8,128)} %sup_x.1, f32[128,256]{1,0:T(8,128)} %sub_y.1, ...), custom_call_target="tpu_custom_call" | custom-call | tf_op jit(solution)/shard_map/reduce/pallas_call | solution.py:457
  23.2 3.4 %finish.1 = f32[128,64,256]{2,1,0:T(8,128)} custom-call(f32[8,128,8,128]{3,2,1,0:T(8,128)S(1)} %get-tuple-element.9.done_a, f32[4,2048,128]{2,1,0:T(8,128)S(1)} %get-tuple-element.10.g_ref, f32[4,8,128]{2,1,0:T(8,128)S(1)} %get-tuple-element.11.edge_ref, f32[256,128]{1,0:T(8,128)S(1)} %get-tuple-element.12.ratio_ref), custom_call_target="tpu_custom_call" | custom-call | tf_op jit(solution)/shard_map/finish/pallas_call | solution.py:484

commit v4 on v3

--- a/solution.py
+++ b/solution.py
@@ -16,8 +16,11 @@
 CB = FB // CH
 CV = CB * JB
 HR = 8
+HW = NJ + 2 * HR
 f32 = jnp.float32
-RL, FL = 44_000_000, 6
+RL, FL = 42_500_000, 6
+LAG = 1
+PITCH = 12
 
 
 def spelled(n, body, state):
@@ -49,7 +52,7 @@
 
             def row(r, gs):
                 j = base + (r if ascending else U - 1 - r)
-                rows = pl.ds(aligned(j * S), S)
+                rows = pl.ds(j * PITCH, S)
                 gs = g_ref[:, rows, :] * bcast(inv_t, j) - bcast(s_t, j) * gs
                 g_ref[:, rows, :] = gs
                 return gs
@@ -71,7 +74,7 @@
 
             def row(r, ws):
                 j = base + (r if ascending else U - 1 - r)
-                rows = pl.ds(aligned(j * S), S)
+                rows = pl.ds(j * PITCH, S)
                 ws = g_ref[:, rows, :] - bcast(ratio_ref, j) * ws
                 g_ref[:, rows, :] = ws
                 return ws
@@ -89,7 +92,7 @@
         view = out_ref.at[fb * JB + jb].reshape(NI * S, L)
 
         def one(f, _):
-            view[pl.ds(f, NI, stride=S), :] = g_ref[fb, pl.ds(jb * L * S + f, L, stride=S), :].T
+            view[pl.ds(f, NI, stride=S), :] = g_ref[fb, pl.ds(jb * L * PITCH + f, L, stride=PITCH), :].T
             return 0
 
         spelled(S, one, 0)
@@ -99,7 +102,7 @@
 
 def reduce_kernel(u_hbm, sub_x, diag_x, sup_x, sub_y, diag_y, sup_y,
                   done_a, g_b, edge_out, ratio_out,
-                  u_in, b1s, b2, b3s, g_a, halo_send, halo_recv,
+                  u_in, b1s, b2, b3s, halo_send, halo_recv,
                   low_x, cen_x, high_x, inv_x, s_x, p_x, f_x, q_x,
                   sy, dy, uy, cen_t, lo_t, hi_t, b_t, a_t, c_t, inv_t, s_t,
                   coef_send, coef_recv, mu_send, mu_recv,
@@ -199,7 +202,7 @@
         def one(f, _):
             parts = [views[jb][pl.ds(f, NI, stride=S), :].T for jb in range(JB)]
             for jb in range(JB):
-                b2[fb * S + f, HR + jb * L:HR + (jb + 1) * L, :] = parts[jb]
+                b2[pl.ds((fb * S + f) * HW + HR + jb * L, L), :] = parts[jb]
             halo_send[pl.ds(fb * S + f, 1), :] = jnp.where(
                 first_y, parts[JB - 1][L - 1:L, :], parts[0][0:1, :])
             return 0
@@ -222,25 +225,33 @@
     ymu_copy = pltpu.make_async_remote_copy(
         ymu_send, ymu_recv, y_ss.at[2], y_rs.at[2], device_id=beside, device_id_type=MESH)
 
+    here = my_x < 4
+    g_a = b2.at[pl.ds(0, HB * NJ * PITCH), :].reshape(HB, NJ * PITCH, L)
+
+    def paced(value, tag):
+        return jnp.where(here, value, tag)
+
     def set_halo(fb):
         def one(f, _):
             halo = halo_recv[pl.ds(fb * S + f, 1), :]
             none = jnp.zeros_like(halo)
-            b2[fb * S + f, HR - 1:HR, :] = jnp.where(first_y, none, halo)
-            b2[fb * S + f, HR + NJ:HR + NJ + 1, :] = jnp.where(first_y, halo, none)
+            b2[pl.ds((fb * S + f) * HW + HR - 1, 1), :] = jnp.where(first_y, none, halo)
+            b2[pl.ds((fb * S + f) * HW + HR + NJ, 1), :] = jnp.where(first_y, halo, none)
             return 0
 
         spelled(S, one, 0)
 
     def stencil(c, h, fs, jb):
         cols = slice(jb * L, (jb + 1) * L)
-        at = HR + jb * L
         cen, lo, hi = cen_t[cols, :], lo_t[cols, :], hi_t[cols, :]
+        tags = []
         for f in fs:
-            f_all = (c * CB + h) * S + f
-            r = (cen * b2[f_all, at:at + L, :] - lo * b2[f_all, at - 1:at - 1 + L, :]
-                 - hi * b2[f_all, at + 1:at + 1 + L, :])
-            b1s[c].at[h, jb].reshape(NI * S, L)[pl.ds(f, NI, stride=S), :] = r.T
+            at = ((c * CB + h) * S + f) * HW + HR + jb * L
+            r = cen * b2[pl.ds(at, L), :] - lo * b2[pl.ds(at - 1, L), :] - hi * b2[pl.ds(at + 1, L), :]
+            rt = r.T
+            b1s[c][h, jb, pl.ds(f, NI, stride=PITCH), :] = rt
+            tags.append(rt[0:S, :])
+        return tags[0]
 
     def fl_copy(c):
         return pltpu.make_async_remote_copy(
@@ -257,7 +268,7 @@
         def row(r, state):
             i = base + r
             g, acc = state
-            g = b1s[c][:, :, i] * bcast_x(inv_x, i) - bcast_x(s_x, i) * g
+            g = b1s[c][:, :, pl.ds(i * PITCH, S), :] * bcast_x(inv_x, i) - bcast_x(s_x, i) * g
             b3s[c][:, :, i] = g
             return g, acc + bcast_x(q_x, i) * g
 
@@ -272,18 +283,21 @@
             if nxt is not None:
                 set_halo(nxt * CB + h)
             span = NI // CB
-            parts = S // 2 * JB
-            n = span // parts
-
-            def part(k, state):
-                for jb in range(JB):
+            n = span // (S // 2)
+
+            def part(k, carry):
+                (g, acc), tag = carry
+                new_tag = tag
+                if c is not None:
                     if nxt is not None:
-                        stencil(nxt, h, (2 * k, 2 * k + 1), jb)
-                    if c is not None:
-                        state = x_forward_rows(c, h * span + (k * JB + jb) * n, n, state)
-                return state
-
-            return spelled(S // 2, part, state)
+                        g = paced(g, tag)
+                    g, acc = x_forward_rows(c, h * span + k * n, n, (g, acc))
+                if nxt is not None:
+                    new_tag = stencil(nxt, h, (2 * k, 2 * k + 1), 0)
+                    stencil(nxt, h, (2 * k, 2 * k + 1), 1)
+                return (g, acc), new_tag
+
+            return spelled(S // 2, part, (state, jnp.zeros((S, L), f32)))[0]
 
         zeros = jnp.zeros((CB, JB, S, L), f32)
         g, acc = lax.fori_loop(0, CB, half, (zeros, zeros))
@@ -342,7 +356,8 @@
         def row(r, w):
             i = base + (n - 1 - r)
             w = b3s[c][:, :, i] + bcast_x(f_x, i) * prev - bcast_x(p_x, i) * w
-            b1s[c][:, :, i] = w + (w - b1s[c][:, :, i])
+            at = pl.ds(i * PITCH, S)
+            b1s[c][:, :, at, :] = w + (w - b1s[c][:, :, at, :])
             return w
 
         return spelled(n, row, w)
@@ -353,18 +368,24 @@
         def half(h, ws):
             span = NI // CB
 
-            def part(f, ws):
-                if c is not None:
-                    ws = x_backward_rows(c, (CB - 1 - h) * span + (S - 1 - f) * (span // S), span // S, prevs, ws)
-                if prior is not None:
-                    g_ref = g_a if prior < HC else g_b
-                    for jb in range(JB):
-                        view = b1s[prior].at[h, jb].reshape(NI * S, L)
-                        g_ref[(prior % HC) * CB + h, pl.ds(jb * L * S + f, L, stride=S), :] = (
-                            view[pl.ds(f, NI, stride=S), :].T)
-                return ws
-
-            return spelled(S, part, ws)
+            n = span // (S * JB)
+
+            def part(f, carry):
+                ws, tags = carry
+                for jb in range(JB):
+                    if c is not None:
+                        if prior is not None:
+                            ws = paced(ws, tags[0])
+                        base = (CB - 1 - h) * span + (S * JB - 1 - f * JB - jb) * n
+                        ws = x_backward_rows(c, base, n, prevs, ws)
+                    if prior is not None:
+                        g_ref = g_a if prior < HC else g_b
+                        cols = b1s[prior][h, jb, pl.ds(f, NI, stride=PITCH), :].T
+                        g_ref[(prior % HC) * CB + h, pl.ds(jb * L * PITCH + f, L, stride=PITCH), :] = cols
+                        tags = tags[1:] + (cols[0:S, :],)
+                return ws, tags
+
+            return spelled(S, part, (ws, (jnp.zeros((S, L), f32),) * LAG))[0]
 
         start = wnext[c] if c is not None else 0
         lax.fori_loop(0, CB, half, start)
@@ -457,14 +478,13 @@
         done, g, edge, ratio = pl.pallas_call(
             reduce_kernel,
             out_shape=(jax.ShapeDtypeStruct((HB * JB, NI, S, L), f32),
-                       jax.ShapeDtypeStruct((HB, NJ * S, L), f32),
+                       jax.ShapeDtypeStruct((HB, NJ * PITCH, L), f32),
                        jax.ShapeDtypeStruct((HB, S, L), f32),
                        jax.ShapeDtypeStruct((NJ, L), f32)),
             in_specs=[hbm] * 7,
             out_specs=(vmem, vmem, vmem, vmem),
             scratch_shapes=[
-                V((FB, JB, NI, S, L), f32), [V((CB, JB, NI, S, L), f32)] * CH, V((NF, NJ + 2 * HR, L), f32), [V((CB, JB, NI, S, L), f32)] * CH,
-                V((HB, NJ * S, L), f32),
+                V((FB, JB, NI, S, L), f32), [V((CB, JB, NI * PITCH, L), f32)] * CH, V((NF * HW, L), f32), [V((CB, JB, NI, S, L), f32)] * CH,
                 V((NF, L), f32), V((NF, L), f32),
                 row_x, row_x, row_x, row_x, row_x, row_x, row_x, row_x,
                 V((NI, NJ), f32), V((NI, NJ), f32), V((NI, NJ), f32),

time: 26.7 us -> 25.3 us (0.948)
  Pallas kernels: 26.6 us -> 25.2 us
    pallas_call x1, Pallas kernels: 23.2 us -> 21.8 us  [local_step(): pl.pallas_call(reduce_kernel, out_shape=(jax.ShapeDtypeStruct((HB * JB, N...]
where the time goes in v4:
time: 25.3 us; the launch traced here: 25.2 us
  Pallas kernels  25.2 us (100%)
    pallas_call x1, Pallas kernels, local_step(): pl.pallas_call(reduce_kernel, out_shape=(jax.ShapeDtypeStruct((HB * JB, N...  21.8 us
    pallas_call x1, Pallas kernels, local_step(): pl.pallas_call(finish_kernel, out_shape=jax.ShapeDtypeStruct((NI, NF, NJ)...  3.42 us

profile of v4, /device:TPU:0, one launch (start us, length us, event | category | flops | bytes accessed | tf_op | source)
XLA Modules:
  0.0 25.2 jit_solution(7774006753817299100)
XLA Ops:
  0.0 21.8 %reduce.1 = (f32[8,128,8,128]{3,2,1,0:T(8,128)S(1)}, f32[4,3072,128]{2,1,0:T(8,128)S(1)}, f32[4,8,128]{2,1,0:T(8,128)S(1)}, f32[256,128]{1,0:T(8,128)S(1)}) custom-call(f32[128,64,256]{2,1,0:T(8,128)} %bitcast.2, f32[128,256]{1,0:T(8,128)} %sub_x.1, f32[128,256]{1,0:T(8,128)} %diag_x.1, f32[128,256]{1,0:T(8,128)} %sup_x.1, f32[128,256]{1,0:T(8,128)} %sub_y.1, ...), custom_call_target="tpu_custom_call" | custom-call | tf_op jit(solution)/shard_map/reduce/pallas_call | solution.py:478
  21.8 3.4 %finish.1 = f32[128,64,256]{2,1,0:T(8,128)} custom-call(f32[8,128,8,128]{3,2,1,0:T(8,128)S(1)} %get-tuple-element.9.done_a, f32[4,3072,128]{2,1,0:T(8,128)S(1)} %get-tuple-element.10.g_ref, f32[4,8,128]{2,1,0:T(8,128)S(1)} %get-tuple-element.11.edge_ref, f32[256,128]{1,0:T(8,128)S(1)} %get-tuple-element.12.ratio_ref), custom_call_target="tpu_custom_call" | custom-call | tf_op jit(solution)/shard_map/finish/pallas_call | solution.py:504
